TPU v7x, 32 devices: a whole 2x2x4 slice. The times are simulated.
32 devices in a mesh: row: 8 (over y, x, core), col: 4 (over z).
Axes of the slice: x: 2, y: 2, z: 4, core: 2. Of those that a mesh axis runs over, the one named last changes fastest.
Arguments:
- points: bfloat16 [4096, 128], P(('row', 'col')), may hold values from -6 to 6
- abar: bfloat16 [4096, 8, 4, 128], P('row', None, 'col'), may hold values from -6 to 6
- inv_scale: float32 [128], replicated, may hold values from 0.05 to 0.2
Outputs:
- point_grad: float32 [4096, 128], P(('row', 'col'))
All inputs are finite; a program needn't handle non-finite values.
Results may differ from a plain program's by a relative error of at most 0.0052.
Values may be sent and summed in bfloat16 or wider, within the bound.
No kernel may reach another device: no remote copies, remote signals or barrier semaphores. Data moves between devices by JAX's collectives and lax.ppermute only.
A program may use at most 64 MiB of HBM per device.

v0:
```python
import jax
import jax.numpy as jnp
from jax import lax
from jax.sharding import PartitionSpec as P


def kernel_weights(left_scaled, left_sq, right_scaled, right_sq, factors):
    inner = lax.dot_general(
        left_scaled, right_scaled, (((1,), (1,)), ((), ())), preferred_element_type=jnp.float32
    )
    dist = left_sq[:, None] + right_sq[None, :] - 2.0 * inner
    return (factors.astype(jnp.float32) * jnp.exp(-0.5 * dist)).astype(jnp.bfloat16)


def per_device(points, abar, inv_scale):
    scaled = (points.astype(jnp.float32) * inv_scale[None, :]).astype(jnp.bfloat16)
    rows_scaled = lax.all_gather(scaled, "col", axis=0, tiled=True)
    cols_scaled = lax.all_gather(scaled, "row", axis=0, tiled=True)
    row_count = rows_scaled.shape[0]
    col_count = cols_scaled.shape[0]
    tile = abar.reshape(row_count, col_count)
    rows_wide = rows_scaled.astype(jnp.float32)
    cols_wide = cols_scaled.astype(jnp.float32)
    rows_sq = jnp.sum(rows_wide * rows_wide, axis=1)
    cols_sq = jnp.sum(cols_wide * cols_wide, axis=1)
    block = 512

    def make_block(index):
        start = index * block
        part_scaled = lax.dynamic_slice_in_dim(rows_scaled, start, block, 0)
        part_sq = lax.dynamic_slice_in_dim(rows_sq, start, block, 0)
        part_ab = lax.dynamic_slice_in_dim(tile, start, block, 0)
        return kernel_weights(part_scaled, part_sq, cols_scaled, cols_sq, part_ab)

    weighted = lax.map(make_block, jnp.arange(row_count // block, dtype=jnp.int32)).reshape(
        row_count, col_count
    )
    part = weighted
    own = rows_wide
    total = jnp.sum(part, axis=1, dtype=jnp.float32)
    first = lax.psum_scatter(
        total[:, None] * own - jnp.dot(part, cols_scaled, preferred_element_type=jnp.float32),
        "col",
        scatter_dimension=0,
        tiled=True,
    )
    part = weighted
    own = cols_wide
    total = jnp.sum(part, axis=0, dtype=jnp.float32)
    product = lax.dot_general(
        part, rows_scaled, (((0,), (0,)), ((), ())), preferred_element_type=jnp.float32
    )
    second = lax.psum_scatter(
        total[:, None] * own - product, "row", scatter_dimension=0, tiled=True
    )
    return -(first + second) * inv_scale[None, :]


def solution(mesh):
    placed = (P(("row", "col"), None), P("row", None, "col", None), P())
    return jax.shard_map(
        per_device, mesh=mesh, in_specs=placed, out_specs=P(("row", "col"), None), check_vma=False
    )
```

profile of v0, /device:TPU:0, one launch (start us, length us, event | category | flops | bytes accessed | tf_op | source)
XLA Modules:
  0.0 100.1 jit_solution(15283611259799010577)
XLA Ops:
  6.5 0.0 reduce-scatter.3.cloned.1.call-start
  6.5 0.8 multiply_convert_fusion
  7.3 15.1 %all_gather.6 = bf16[512,128]{1,0:T(8,128)(2,1)S(1)} all-gather(bf16[128,128]{1,0:T(8,128)(2,1)S(1)} %multiply_convert_fusion), channel_id=1, replica_groups=mesh['row'=8,'col'=4] {'col'}, dimensions={0}, use_global_device_ids=true | all-gather | bytes 163840 | tf_op jit(solution)/shard_map/all_gather | solution.py:17
  22.4 9.3 %all_gather.7 = bf16[1024,128]{1,0:T(8,128)(2,1)S(1)} all-gather(bf16[128,128]{1,0:T(8,128)(2,1)S(1)} %multiply_convert_fusion), channel_id=1, replica_groups=mesh['row'=8,'col'=4] {'row'}, dimensions={0}, use_global_device_ids=true | all-gather | bytes 294912 | tf_op jit(solution)/shard_map/all_gather | solution.py:18
  31.7 0.1 fusion.2
  31.8 0.2 fusion.1
  32.1 1.5 %convert.1 = f32[64,8,8,128]{3,2,1,0:T(8,128)S(1)} convert(bf16[64,8,8,128]{3,2,1,0:T(8,128)(2,1)} %bitcast.14) | non-fusion elementwise | flops 524288 | bytes 3145728
  33.5 1.0 %convert_reduce_fusion = (f32[1024]{0:T(1024)S(1)}, f32[512]{0:T(512)S(1)}, bf16[512,1024]{1,0:T(8,128)(2,1)S(1)}) fusion(bf16[512,128]{1,0:T(8,128)(2,1)S(1)} %all_gather.6, bf16[1024,128]{1,0:T(8,128)(2,1)S(1)} %all_gather.7, f32[1024]{0:T(1024)S(1)} %fusion.1, f32[512]{0:T(512)S(1)} %fusion.2, f32[64,8,8,128]{3,2,1,0:T(8,128)S(1)} %convert.1), kind=kOutput, calls=%fused_computation | convolution fusion | flops 138934784 | bytes 3551232 | tf_op jit(solution)/shard_map/while/body/eval_jaxpr/dot_general | solution.py:8
  34.6 0.0 copy-start
  34.6 1.2 %convolution_subtract_fusion.1 = f32[512,128]{1,0:T(8,128)} fusion(bf16[512,1024]{1,0:T(8,128)(2,1)S(1)} %get-tuple-element.19, bf16[1024,128]{1,0:T(8,128)(2,1)S(1)} %all_gather.7, bf16[512,128]{1,0:T(8,128)(2,1)S(1)} %all_gather.6, f32[512]{0:T(512)S(1)} %get-tuple-element.18), kind=kOutput, calls=%fused_computation.5 | convolution fusion | flops 134414336 | bytes 1705984 | tf_op jit(solution)/shard_map/dot_general | solution.py:42
  35.7 0.0 reduce-scatter.3.cloned.1.call-update
  35.8 0.0 reduce-scatter.5.cloned.1.call-start
  35.8 1.3 %convolution_subtract_fusion = f32[1024,128]{1,0:T(8,128)} fusion(bf16[512,1024]{1,0:T(8,128)(2,1)S(1)} %get-tuple-element.19, bf16[512,128]{1,0:T(8,128)(2,1)S(1)} %all_gather.6, bf16[1024,128]{1,0:T(8,128)(2,1)S(1)} %all_gather.7, f32[1024]{0:T(1024)S(1)} %get-tuple-element.17), kind=kOutput, calls=%fused_computation.4 | convolution fusion | flops 134610944 | bytes 1970176 | tf_op jit(solution)/shard_map/dot_general | solution.py:50
  37.1 0.0 reduce-scatter.5.cloned.1.call-update
  37.1 19.2 %reduce-scatter.3.cloned.1.call-done = f32[128,128]{1,0:T(8,128)} async-done(((f32[512,128]{1,0:T(8,128)}), f32[128,128]{1,0:T(8,128)}) %reduce-scatter.3.cloned.1.call-update) | async-done | bytes 65552 | tf_op jit(solution)/shard_map/reduce_scatter | solution.py:41
  56.3 35.5 %reduce-scatter.5.cloned.1.call-done = f32[128,128]{1,0:T(8,128)} async-done(((f32[1024,128]{1,0:T(8,128)}), f32[128,128]{1,0:T(8,128)}) %reduce-scatter.5.cloned.1.call-update) | async-done | bytes 65552 | tf_op jit(solution)/shard_map/reduce_scatter | solution.py:53
  91.8 0.0 copy-done
  91.8 1.5 %negate_multiply_fusion = f32[128,128]{1,0:T(8,128)} fusion(f32[128,128]{1,0:T(8,128)} %reduce-scatter.3.cloned.1.call-done, f32[128,128]{1,0:T(8,128)} %reduce-scatter.5.cloned.1.call-done, f32[128]{0:T(128)S(1)} %copy-done), kind=kLoop, calls=%fused_computation.12 | loop fusion | flops 49152 | bytes 197120 | tf_op jit(solution)/shard_map/mul | solution.py:56
Async XLA Ops:
  6.5 49.8 %reduce-scatter.3.cloned.1.call-start = ((), (), s32[]{:S(2)}) async-start(), calls=%async_computation.2 | async-start | bytes 327680 | tf_op jit(solution)/shard_map/reduce_scatter | solution.py:41
  34.6 57.2 %copy-start = (f32[128]{0:T(128)S(1)}, f32[128]{0:T(128)}, u32[]{:S(2)}) copy-start(f32[128]{0:T(128)} %param.5) | copy-start | bytes 1540
  35.8 56.0 %reduce-scatter.5.cloned.1.call-start = ((), (), s32[]{:S(2)}) async-start(), calls=%async_computation.3 | async-start | bytes 589824 | tf_op jit(solution)/shard_map/reduce_scatter | solution.py:53
Sparse Core Ops, SparseCore 0:
  35.9 20.3 reduce-scatter.2
  59.4 32.3 reduce-scatter.4
where the time goes:
time: 100 us
  waiting for transfers between devices  54.7 us (55%)
  blocking collectives  24.4 us (24%)
  between operations  13.4 us (13%)
  other arithmetic  4.11 us (4%)
  matrix products  3.48 us (3%)
    reduce_scatter x1, waiting for transfers between devices, per_device(): lax.psum_scatter(total[:, None] * own - product, 'row', scatter_dimension...  35.5 us
    reduce_scatter x1, waiting for transfers between devices, per_device(): lax.psum_scatter(total[:, None] * own - jnp.dot(part, cols_scaled, prefer...  19.2 us
    all_gather x1, blocking collectives, per_device(): rows_scaled = lax.all_gather(scaled, 'col', axis=0, tiled=True)  15.1 us
    all_gather x1, blocking collectives, per_device(): cols_scaled = lax.all_gather(scaled, 'row', axis=0, tiled=True)  9.29 us
  transfers between devices with their start and end apart: 2, of which 2 were waited for; matrix products, arithmetic and copies ran while one was open for 1% of the time, Pallas kernels for 0%

commit v1 on v0

v1 whole, which is shorter than its diff:
```python
import jax
import jax.numpy as jnp
from jax import lax
from jax.experimental import pallas as pl
from jax.experimental.pallas import tpu as pltpu
from jax.sharding import PartitionSpec as P


F32, BF16 = jnp.float32, jnp.bfloat16
AXES = ("row", "col")
VMEM = pl.BlockSpec(memory_space=pltpu.VMEM)
OVER_LAST, OVER_FIRST, PLAIN = ((1,), (1,)), ((0,), (0,)), ((1,), (0,))


def partner(i, distance, n):
    return i ^ distance if n & (n - 1) == 0 else (i + distance) % n


def origin(i, distance, n):
    return i ^ distance if n & (n - 1) == 0 else lax.rem(i + n - distance, n)


def dot(a, b, over):
    return lax.dot_general(a, b, (over, ((), ())), preferred_element_type=F32)


def augmented(raw, inv, first):
    s = (raw.astype(F32) * inv).astype(BF16)
    wide = s.astype(F32)
    rest = -0.5 * jnp.sum(wide * wide, axis=1, keepdims=True)
    lane = lax.broadcasted_iota(jnp.int32, s.shape, 1)
    tail = jnp.zeros(s.shape, F32)
    for n in range(3):
        piece = rest.astype(BF16).astype(F32)
        rest = rest - piece
        tail = jnp.where(lane == (n if first else n + 3), piece, tail)
        tail = jnp.where(lane == (n + 3 if first else n), 1.0, tail)
    return jnp.concatenate([s, tail.astype(BF16)], 1)


class Layout:
    def __init__(self, lines, planes, pts, width):
        self.lines, self.planes, self.pts, self.width = lines, planes, pts, width
        self.steps = max(lines, planes) - 1
        self.chip = 2 * pts

    def distance(self, k):
        return self.steps + 1 - k

    def valid(self, k, n):
        return k == 0 or self.distance(k) < n

    def here(self):
        row = lax.axis_index("row")
        return lax.axis_index("col"), lax.div(row, 2), lax.rem(row, 2)

    def rows(self, k):
        return slice(k * self.chip, (k + 1) * self.chip)

    def weights(self, tiles, line, plane, exponent):
        at = pl.ds(pl.multiple_of(line * self.pts, self.pts), self.pts)
        cols = pl.ds(pl.multiple_of(plane * self.chip, self.chip), self.chip)
        a = jnp.concatenate([tile[at, cols] for tile in tiles], 0)
        return (a.astype(F32) * jnp.exp(exponent)).astype(BF16)

    def term(self, core, tiles, mine, mine_at, theirs, theirs_at):
        side = jnp.concatenate([theirs[:, : self.width], jnp.ones((self.chip, self.width), BF16)], 1)
        if core:
            w = self.weights(tiles, mine_at, theirs_at, dot(mine, theirs, OVER_LAST))
            return dot(w, side, PLAIN)
        w = self.weights(tiles, theirs_at, mine_at, dot(theirs, mine, OVER_LAST))
        return dot(w, side, OVER_FIRST)

    def on_each_core(self, body):
        line, plane, core = self.here()
        for c in (0, 1):
            own, other = ((plane, self.planes), (line, self.lines))[:: 1 if c == 0 else -1]

            @pl.when(core == c)
            def _(c=c, own=own, other=other):
                body(c, *own, *other)

    def early(self, chip, inv, near, a_own, a_other, mine, part):
        def body(core, own, own_n, other, other_n):
            tiles = (a_other, a_own) if core else (a_own, a_other)
            theirs = augmented(chip[...], inv[...], not core)
            for k in range(self.steps + 1):
                if not self.valid(k, own_n):
                    continue
                raw = near[self.rows(k - 1), :] if k else chip[...]
                block = augmented(raw, inv[...], bool(core))
                mine[self.rows(k), :] = block
                at = origin(own, self.distance(k), own_n) if k else own
                part[self.rows(k), :] = self.term(core, tiles, block, at, theirs, other)

        self.on_each_core(body)

    def finished(self, k, core, tiles, theirs, mine, part, own, own_n, other, other_n):
        block = mine[self.rows(k), :]
        at = origin(own, self.distance(k), own_n) if k else own
        total = part[self.rows(k), :]
        for j in range(1, self.steps + 1):
            if self.valid(j, other_n):
                from_at = origin(other, self.distance(j), other_n)
                total += self.term(core, tiles, block, at, theirs[self.rows(j - 1), :], from_at)
        return total[:, self.width :] * block[:, : self.width].astype(F32) - total[:, : self.width]

    def send(self, far, inv, mine, part, a_own, a_other, theirs, *outs):
        def body(core, own, own_n, other, other_n):
            tiles = (a_other, a_own) if core else (a_own, a_other)
            for j in range(1, self.steps + 1):
                if self.valid(j, other_n):
                    theirs[self.rows(j - 1), :] = augmented(far[self.rows(j - 1), :], inv[...], not core)
            for k in range(1, self.steps + 1):
                out = outs[k - 1]
                if self.valid(k, own_n):
                    value = self.finished(k, core, tiles, theirs, mine, part, own, own_n, other, other_n)
                    out[...] = value.astype(out.dtype)
                else:
                    out[...] = jnp.zeros(out.shape, out.dtype)

        self.on_each_core(body)

    def keep(self, theirs, mine, part, a_own, a_other, out):
        def body(core, own, own_n, other, other_n):
            tiles = (a_other, a_own) if core else (a_own, a_other)
            out[...] = self.finished(0, core, tiles, theirs, mine, part, own, own_n, other, other_n)

        self.on_each_core(body)

    def total(self, *refs):
        terms, (keep, send) = refs[:-2], refs[-2:]
        core = self.here()[2]
        mine = pl.ds(pl.multiple_of(core * self.pts, self.pts), self.pts)
        other = pl.ds(pl.multiple_of((1 - core) * self.pts, self.pts), self.pts)
        for ref, rows in ((keep, mine), (send, other)):
            acc = terms[0][rows, :].astype(F32)
            for term in terms[1:]:
                acc += term[rows, :].astype(F32)
            ref[...] = acc


def solution(mesh):
    rows, lines = mesh.shape["row"], mesh.shape["col"]
    planes = rows // 2
    steps = max(lines, planes) - 1

    def permute(value, target):
        pairs = []
        for r in range(rows):
            for c in range(lines):
                tr, tc = target(r, c)
                pairs.append((r * lines + c, tr * lines + tc))
        return lax.ppermute(value, AXES, pairs)

    def swap(value):
        return permute(value, lambda r, c: (r ^ 1, c))

    def exchange(value, k):
        distance = steps + 1 - k

        def target(r, c):
            if r % 2:
                return r, partner(c, (distance - 1) % (lines - 1) + 1, lines)
            return 2 * partner(r // 2, (distance - 1) % (planes - 1) + 1, planes), c

        return permute(value, target)

    def local_part(points, abar, inv_scale):
        pts, width = points.shape
        lay = Layout(lines, planes, pts, width)
        chip_rows = lay.chip
        core = lax.axis_index("row") % 2
        inv = inv_scale[None, :]
        grant = pltpu.CompilerParams(vmem_limit_bytes=(6 + steps) * 2**20)

        def call(body, outs, *args):
            return pl.pallas_call(
                body,
                out_shape=[jax.ShapeDtypeStruct(s, t) for s, t in outs],
                in_specs=[VMEM] * len(args),
                out_specs=[VMEM] * len(outs),
                compiler_params=grant,
            )(*args)

        other = swap(points)
        abar_other = swap(abar)
        chip = lax.dynamic_update_slice(
            jnp.zeros((chip_rows, width), points.dtype), points, (core * pts, 0)
        )
        chip = lax.dynamic_update_slice(chip, other, ((1 - core) * pts, 0))
        near = []
        for k in range(1, steps + 1):
            near.append(exchange(chip, k))
        abar, _ = lax.optimization_barrier((abar, chip))
        tiles = [a.reshape(a.shape[0], -1).astype(F32) for a in (abar, abar_other)]
        near = jnp.concatenate(near, 0)
        far = swap(near)
        blocks = (steps + 1) * chip_rows
        mine, part = call(lay.early, [((blocks, 2 * width), BF16), ((blocks, 2 * width), F32)], chip, inv, near, *tiles)
        theirs, *outs = call(
            lay.send,
            [((steps * chip_rows, 2 * width), BF16)] + [((chip_rows, width), BF16)] * steps,
            far,
            inv,
            mine,
            part,
            *tiles,
        )
        got = []
        for k in range(1, steps + 1):
            got.append(exchange(outs[k - 1], k))
        (out,) = call(lay.keep, [((chip_rows, width), F32)], theirs, mine, part, *tiles)
        keep, send = call(lay.total, [((pts, width), F32)] * 2, out, *got)
        return -(keep + swap(send)) * inv

    placed = (P(("row", "col"), None), P("row", None, "col", None), P())
    return jax.shard_map(local_part, mesh=mesh, in_specs=placed, out_specs=P(("row", "col"), None), check_vma=False)
```

time: 100 us -> 26.2 us (0.26)
  waiting for transfers between devices: 54.7 us -> 10 us
  blocking collectives: 24.4 us -> 0 us
  between operations: 13.4 us -> 0.1 us
  starting transfers between devices: 0.04 us -> 8.87 us
  matrix products: 3.48 us -> 0 us
  other arithmetic: 4.11 us -> 0.64 us
  Pallas kernels: 0 us -> 3.45 us
  local copies, waits for them, and re-layouts: 0.01 us -> 2.94 us
    reduce_scatter x2 -> x0, waiting for transfers between devices: 54.6 us -> none  [the longest x1 35.5 us: per_device(): lax.psum_scatter(total[:, None] * own - product, 'row', scatter_dimension...]
    all_gather x2 -> x0, blocking collectives: 24.4 us -> none  [the longest x1 15.1 us: per_device(): rows_scaled = lax.all_gather(scaled, 'col', axis=0, tiled=True)]
    ppermute x0 -> x10, waiting for transfers between devices: none -> 10 us  [permute(): return lax.ppermute(value, AXES, pairs)]
    ppermute x0 -> x10, starting transfers between devices: none -> 8.87 us  [permute(): return lax.ppermute(value, AXES, pairs)]
    dot_general x3 -> x0, matrix products: 3.48 us -> none  [the longest x1 1.28 us: per_device(): lax.dot_general(part, rows_scaled, (((0,), (0,)), ((), ())), preferred_el...]
    pallas_call x0 -> x4, Pallas kernels: none -> 3.45 us  [call(): pl.pallas_call(body, out_shape=[jax.ShapeDtypeStruct(s, t) for s, t in ou...]
    unnamed x2 -> x6, local copies, waits for them, and re-layouts: 0.01 us -> 2.14 us
    unnamed x1 -> x0, other arithmetic: 1.47 us -> none
  transfers between devices with their start and end apart: 2 -> 10, of which waited for: 2 -> 7; matrix products, arithmetic and copies ran while one was open for 1% -> 10% of each run, Pallas kernels for 0% -> 7%
where the time goes in v1:
time: 26.2 us; the launch traced here: 26 us
  waiting for transfers between devices  10 us (38%)
  starting transfers between devices  8.87 us (34%)
  Pallas kernels  3.45 us (13%)
  local copies, waits for them, and re-layouts  2.94 us (11%)
  other arithmetic  0.64 us (2%)
    ppermute x10, waiting for transfers between devices, permute(): return lax.ppermute(value, AXES, pairs)  10 us
    ppermute x10, starting transfers between devices, permute(): return lax.ppermute(value, AXES, pairs)  8.87 us
    pallas_call x4, Pallas kernels, call(): pl.pallas_call(body, out_shape=[jax.ShapeDtypeStruct(s, t) for s, t in ou...  3.45 us
    unnamed x6, local copies, waits for them, and re-layouts  2.14 us
    dynamic_update_slice x1, local copies, waits for them, and re-layouts, local_part(): lax.dynamic_update_slice(jnp.zeros((chip_rows, width), points.dtype), poi...  0.77 us
    mul x1, other arithmetic, local_part(): return -(keep + swap(send)) * inv  0.64 us
  transfers between devices with their start and end apart: 10, of which 7 were waited for; matrix products, arithmetic and copies ran while one was open for 10% of the time, Pallas kernels for 7%

profile of v1, /device:TPU:0, one launch (start us, length us, event | category | flops | bytes accessed | tf_op | source)
XLA Modules:
  0.0 26.0 jit_solution(16703110679349333661)
XLA Ops:
  0.0 0.5 %collective-permute-start.5 = (bf16[512,8,1,128]{3,1,2,0:T(8,128)(2,1)}, bf16[512,8,1,128]{3,1,2,0:T(8,128)(2,1)S(1)}, u32[]{:S(2)}, u32[]{:S(2)}) collective-permute-start(bf16[512,8,1,128]{3,1,2,0:T(8,128)(2,1)} %param.4), channel_id=1, source_target_pairs={{0,4},{1,5},{2,6},{3,7},{4,0},{5,1},{6,2},{7,3},{8,12},{9,13},{10,... | collective-permute-start | bytes 3145736 | tf_op jit(solution)/shard_map/ppermute | solution.py:154
  0.5 0.0 collective-permute-start
  0.5 0.8 %constant_dynamic-update-slice_fusion.4 = bf16[256,128]{1,0:T(8,128)(2,1)S(1)} fusion(bf16[256,128]{1,0:T(8,128)(2,1)S(1)} %broadcast_in_dim.6, bf16[128,128]{1,0:T(8,128)(2,1)} %param.3, s32[]{:T(128)S(6)} %select_n.14), kind=kLoop, calls=%fused_computation.7 | loop fusion | bytes 65540 | tf_op jit(solution)/shard_map/dynamic_update_slice | solution.py:188
  1.3 1.7 %collective-permute-done = bf16[128,128]{1,0:T(8,128)(2,1)S(1)} collective-permute-done((bf16[128,128]{1,0:T(8,128)(2,1)}, bf16[128,128]{1,0:T(8,128)(2,1)S(1)}, u32[]{:S(2)}, u32[]{:S(2)}) %collective-permute-start) | collective-permute-done | bytes 32800 | tf_op jit(solution)/shard_map/ppermute | solution.py:154
  3.0 3.8 %collective-permute-start.1 = (bf16[256,128]{1,0:T(8,128)(2,1)S(1)}, bf16[256,128]{1,0:T(8,128)(2,1)S(1)}, u32[]{:S(2)}, u32[]{:S(2)}) collective-permute-start(bf16[256,128]{1,0:T(8,128)(2,1)S(1)} %constant_dynamic-update-slice_fusion.3.chip), channel_id=1, source_target_pairs={{0,24},{1,25},{2,26},{3,27},{4,7},{5,6},{6,5},{7,4},{8,16},{9,17},... | collective-permute-start | bytes 196616 | tf_op jit(solution)/shard_map/ppermute | solution.py:154
  6.9 0.5 %collective-permute-start.3 = (bf16[256,128]{1,0:T(8,128)(2,1)S(1)}, bf16[256,128]{1,0:T(8,128)(2,1)S(1)}, u32[]{:S(2)}, u32[]{:S(2)}) collective-permute-start(bf16[256,128]{1,0:T(8,128)(2,1)S(1)} %constant_dynamic-update-slice_fusion.3.chip), channel_id=1, source_target_pairs={{0,8},{1,9},{2,10},{3,11},{4,5},{5,4},{6,7},{7,6},{8,0},{9,1},{10,... | collective-permute-start | bytes 196616 | tf_op jit(solution)/shard_map/ppermute | solution.py:154
  7.4 0.1 collective-permute-start.2
  7.5 1.6 %collective-permute-done.1 = bf16[256,128]{1,0:T(8,128)(2,1)S(1)} collective-permute-done((bf16[256,128]{1,0:T(8,128)(2,1)S(1)}, bf16[256,128]{1,0:T(8,128)(2,1)S(1)}, u32[]{:S(2)}, u32[]{:S(2)}) %collective-permute-start.1) | collective-permute-done | bytes 65568 | tf_op jit(solution)/shard_map/ppermute | solution.py:154
  9.1 2.6 %collective-permute-done.2 = bf16[256,128]{1,0:T(8,128)(2,1)S(1)} collective-permute-done((bf16[256,128]{1,0:T(8,128)(2,1)S(1)}, bf16[256,128]{1,0:T(8,128)(2,1)S(1)}, u32[]{:S(2)}, u32[]{:S(2)}) %collective-permute-start.2) | collective-permute-done | bytes 65568 | tf_op jit(solution)/shard_map/ppermute | solution.py:154
  11.7 0.0 collective-permute-done.3
  11.7 0.3 %collective-permute-start.4 = (bf16[768,128]{1,0:T(8,128)(2,1)S(1)}, bf16[768,128]{1,0:T(8,128)(2,1)S(1)}, u32[]{:S(2)}, u32[]{:S(2)}) collective-permute-start(bf16[768,128]{1,0:T(8,128)(2,1)S(1)} %constant_dynamic-update-slice_fusion.near), channel_id=1, source_target_pairs={{0,4},{1,5},{2,6},{3,7},{4,0},{5,1},{6,2},{7,3},{8,12},{9,13},{10,... | collective-permute-start | bytes 589832 | tf_op jit(solution)/shard_map/ppermute | solution.py:154
  12.0 1.5 %copy.9 = f32[64,8,8,128]{3,1,2,0:T(8,128)S(1)} copy(bf16[64,8,8,128]{3,2,1,0:T(8,128)(2,1)} %bitcast.23) | data formatting | bytes 3145728
  13.5 0.0 copy-start
  13.5 0.0 collective-permute-done.5
  13.5 0.3 %copy.8 = f32[64,8,8,128]{3,1,2,0:T(8,128)S(1)} copy(bf16[64,8,8,128]{3,2,1,0:T(8,128)(2,1)S(1)} %bitcast.24) | data formatting | bytes 3145728
  13.8 0.4 %copy-done = f32[128]{0:T(128)S(1)} copy-done((f32[128]{0:T(128)S(1)}, f32[128]{0:T(128)}, u32[]{:S(2)}) %copy-start) | copy-done | bytes 536
  14.1 1.0 %shard_map.37 = (bf16[1024,256]{1,0:T(8,128)(2,1)S(1)}, f32[1024,256]{1,0:T(8,128)S(1)}) custom-call(bf16[256,128]{1,0:T(8,128)(2,1)S(1)} %constant_dynamic-update-slice_fusion.3.chip, f32[1,128]{1,0:T(1,128)S(1)} %bitcast.21, bf16[768,128]{1,0:T(8,128)(2,1)S(1)} %constant_dynamic-update-slice_fusion.near, f32[512,1024]{1,0:T(8,128)S(1)} %bitcast.15, ...), custom_call_target="tpu_custom_call" | custom-call | tf_op jit(solution)/shard_map/pallas_call | solution.py:178
  15.2 0.0 collective-permute-done.4.far
  15.2 1.5 %shard_map.38 = (bf16[768,256]{1,0:T(8,128)(2,1)S(1)}, bf16[256,128]{1,0:T(8,128)(2,1)S(1)}, bf16[256,128]{1,0:T(8,128)(2,1)S(1)}, bf16[256,128]{1,0:T(8,128)(2,1)S(1)}) custom-call(bf16[768,128]{1,0:T(8,128)(2,1)S(1)} %collective-permute-done.4.far, f32[1,128]{1,0:T(1,128)S(1)} %bitcast.22, bf16[1024,256]{1,0:T(8,128)(2,1)S(1)} %get-tuple-element.15.mine, ...), custom_call_target="tpu_custom_call" | custom-call | tf_op jit(solution)/shard_map/pallas_call | solution.py:178
  16.8 2.5 %collective-permute-start.6 = (bf16[256,128]{1,0:T(8,128)(2,1)S(1)}, bf16[256,128]{1,0:T(8,128)(2,1)S(1)}, u32[]{:S(2)}, u32[]{:S(2)}) collective-permute-start(bf16[256,128]{1,0:T(8,128)(2,1)S(1)} %get-tuple-element.18), channel_id=1, source_target_pairs={{0,24},{1,25},{2,26},{3,27},{4,7},{5,6},{6,5},{7,4},{8,16},{9,17},... | collective-permute-start | bytes 196616 | tf_op jit(solution)/shard_map/ppermute | solution.py:154
  19.3 0.5 %collective-permute-start.7 = (bf16[256,128]{1,0:T(8,128)(2,1)S(1)}, bf16[256,128]{1,0:T(8,128)(2,1)S(1)}, u32[]{:S(2)}, u32[]{:S(2)}) collective-permute-start(bf16[256,128]{1,0:T(8,128)(2,1)S(1)} %get-tuple-element.19), channel_id=1, source_target_pairs={{0,16},{1,17},{2,18},{3,19},{4,6},{5,7},{6,4},{7,5},{8,24},{9,25},... | collective-permute-start | bytes 196616 | tf_op jit(solution)/shard_map/ppermute | solution.py:154
  19.8 0.5 %collective-permute-start.8 = (bf16[256,128]{1,0:T(8,128)(2,1)S(1)}, bf16[256,128]{1,0:T(8,128)(2,1)S(1)}, u32[]{:S(2)}, u32[]{:S(2)}) collective-permute-start(bf16[256,128]{1,0:T(8,128)(2,1)S(1)} %get-tuple-element.20), channel_id=1, source_target_pairs={{0,8},{1,9},{2,10},{3,11},{4,5},{5,4},{6,7},{7,6},{8,0},{9,1},{10,... | collective-permute-start | bytes 196616 | tf_op jit(solution)/shard_map/ppermute | solution.py:154
  20.3 0.8 %shard_map.39.refs_0_ = f32[256,128]{1,0:T(8,128)S(1)} custom-call(bf16[768,256]{1,0:T(8,128)(2,1)S(1)} %get-tuple-element.17.theirs, bf16[1024,256]{1,0:T(8,128)(2,1)S(1)} %get-tuple-element.15.mine, f32[1024,256]{1,0:T(8,128)S(1)} %get-tuple-element.16.part, f32[512,1024]{1,0:T(8,128)S(1)} %bitcast.17, f32[512,1024]{1,0:T(8,128)S(1)} %bitcast.20), custom_call_target="tpu_custom_call" | custom-call | tf_op jit(solution)/shard_map/pallas_call | solution.py:178
  21.1 0.8 %collective-permute-done.6.refs_1_ = bf16[256,128]{1,0:T(8,128)(2,1)S(1)} collective-permute-done((bf16[256,128]{1,0:T(8,128)(2,1)S(1)}, bf16[256,128]{1,0:T(8,128)(2,1)S(1)}, u32[]{:S(2)}, u32[]{:S(2)}) %collective-permute-start.6) | collective-permute-done | bytes 65568 | tf_op jit(solution)/shard_map/ppermute | solution.py:154
  22.0 1.5 %collective-permute-done.7.refs_2_ = bf16[256,128]{1,0:T(8,128)(2,1)S(1)} collective-permute-done((bf16[256,128]{1,0:T(8,128)(2,1)S(1)}, bf16[256,128]{1,0:T(8,128)(2,1)S(1)}, u32[]{:S(2)}, u32[]{:S(2)}) %collective-permute-start.7) | collective-permute-done | bytes 65568 | tf_op jit(solution)/shard_map/ppermute | solution.py:154
  23.5 0.5 %collective-permute-done.8.refs_3_ = bf16[256,128]{1,0:T(8,128)(2,1)S(1)} collective-permute-done((bf16[256,128]{1,0:T(8,128)(2,1)S(1)}, bf16[256,128]{1,0:T(8,128)(2,1)S(1)}, u32[]{:S(2)}, u32[]{:S(2)}) %collective-permute-start.8) | collective-permute-done | bytes 65568 | tf_op jit(solution)/shard_map/ppermute | solution.py:154
  24.1 0.1 collective-permute-start.9
  24.1 1.2 %collective-permute-done.9 = f32[128,128]{1,0:T(8,128)S(1)} collective-permute-done((f32[128,128]{1,0:T(8,128)S(1)}, f32[128,128]{1,0:T(8,128)S(1)}, u32[]{:S(2)}, u32[]{:S(2)}) %collective-permute-start.9) | collective-permute-done | bytes 65568 | tf_op jit(solution)/shard_map/ppermute | solution.py:154
  25.4 0.6 %negate_multiply_fusion = f32[128,128]{1,0:T(8,128)} fusion(f32[128,128]{1,0:T(8,128)S(1)} %get-tuple-element.21, f32[128,128]{1,0:T(8,128)S(1)} %collective-permute-done.9, f32[128]{0:T(128)S(1)} %copy-done), kind=kLoop, calls=%fused_computation.2 | loop fusion | flops 49152 | bytes 197120 | tf_op jit(solution)/shard_map/mul | solution.py:215
  (6 shorter events, 0.1 us)
Async XLA Ops:
  0.0 13.5 %collective-permute-start.5 = (bf16[512,8,1,128]{3,1,2,0:T(8,128)(2,1)}, bf16[512,8,1,128]{3,1,2,0:T(8,128)(2,1)S(1)}, u32[]{:S(2)}, u32[]{:S(2)}) collective-permute-start(bf16[512,8,1,128]{3,1,2,0:T(8,128)(2,1)} %param.4), channel_id=1, source_target_pairs={{0,4},{1,5},{2,6},{3,7},{4,0},{5,1},{6,2},{7,3},{8,12},{9,13},{10,... | collective-permute-start | bytes 3145736 | tf_op jit(solution)/shard_map/ppermute | solution.py:154
  0.5 2.5 %collective-permute-start = (bf16[128,128]{1,0:T(8,128)(2,1)}, bf16[128,128]{1,0:T(8,128)(2,1)S(1)}, u32[]{:S(2)}, u32[]{:S(2)}) collective-permute-start(bf16[128,128]{1,0:T(8,128)(2,1)} %param.3), channel_id=1, source_target_pairs={{0,4},{1,5},{2,6},{3,7},{4,0},{5,1},{6,2},{7,3},{8,12},{9,13},{10,... | collective-permute-start | bytes 98312 | tf_op jit(solution)/shard_map/ppermute | solution.py:154
  3.0 6.0 %collective-permute-start.1 = (bf16[256,128]{1,0:T(8,128)(2,1)S(1)}, bf16[256,128]{1,0:T(8,128)(2,1)S(1)}, u32[]{:S(2)}, u32[]{:S(2)}) collective-permute-start(bf16[256,128]{1,0:T(8,128)(2,1)S(1)} %constant_dynamic-update-slice_fusion.3.chip), channel_id=1, source_target_pairs={{0,24},{1,25},{2,26},{3,27},{4,7},{5,6},{6,5},{7,4},{8,16},{9,17},... | collective-permute-start | bytes 196616 | tf_op jit(solution)/shard_map/ppermute | solution.py:154
  6.9 4.8 %collective-permute-start.3 = (bf16[256,128]{1,0:T(8,128)(2,1)S(1)}, bf16[256,128]{1,0:T(8,128)(2,1)S(1)}, u32[]{:S(2)}, u32[]{:S(2)}) collective-permute-start(bf16[256,128]{1,0:T(8,128)(2,1)S(1)} %constant_dynamic-update-slice_fusion.3.chip), channel_id=1, source_target_pairs={{0,8},{1,9},{2,10},{3,11},{4,5},{5,4},{6,7},{7,6},{8,0},{9,1},{10,... | collective-permute-start | bytes 196616 | tf_op jit(solution)/shard_map/ppermute | solution.py:154
  7.4 4.3 %collective-permute-start.2 = (bf16[256,128]{1,0:T(8,128)(2,1)S(1)}, bf16[256,128]{1,0:T(8,128)(2,1)S(1)}, u32[]{:S(2)}, u32[]{:S(2)}) collective-permute-start(bf16[256,128]{1,0:T(8,128)(2,1)S(1)} %constant_dynamic-update-slice_fusion.3.chip), channel_id=1, source_target_pairs={{0,16},{1,17},{2,18},{3,19},{4,6},{5,7},{6,4},{7,5},{8,24},{9,25},... | collective-permute-start | bytes 196616 | tf_op jit(solution)/shard_map/ppermute | solution.py:154
  11.7 3.5 %collective-permute-start.4 = (bf16[768,128]{1,0:T(8,128)(2,1)S(1)}, bf16[768,128]{1,0:T(8,128)(2,1)S(1)}, u32[]{:S(2)}, u32[]{:S(2)}) collective-permute-start(bf16[768,128]{1,0:T(8,128)(2,1)S(1)} %constant_dynamic-update-slice_fusion.near), channel_id=1, source_target_pairs={{0,4},{1,5},{2,6},{3,7},{4,0},{5,1},{6,2},{7,3},{8,12},{9,13},{10,... | collective-permute-start | bytes 589832 | tf_op jit(solution)/shard_map/ppermute | solution.py:154
  13.5 0.7 %copy-start = (f32[128]{0:T(128)S(1)}, f32[128]{0:T(128)}, u32[]{:S(2)}) copy-start(f32[128]{0:T(128)} %param.5) | copy-start | bytes 1540
  16.8 5.2 %collective-permute-start.6 = (bf16[256,128]{1,0:T(8,128)(2,1)S(1)}, bf16[256,128]{1,0:T(8,128)(2,1)S(1)}, u32[]{:S(2)}, u32[]{:S(2)}) collective-permute-start(bf16[256,128]{1,0:T(8,128)(2,1)S(1)} %get-tuple-element.18), channel_id=1, source_target_pairs={{0,24},{1,25},{2,26},{3,27},{4,7},{5,6},{6,5},{7,4},{8,16},{9,17},... | collective-permute-start | bytes 196616 | tf_op jit(solution)/shard_map/ppermute | solution.py:154
  19.3 4.3 %collective-permute-start.7 = (bf16[256,128]{1,0:T(8,128)(2,1)S(1)}, bf16[256,128]{1,0:T(8,128)(2,1)S(1)}, u32[]{:S(2)}, u32[]{:S(2)}) collective-permute-start(bf16[256,128]{1,0:T(8,128)(2,1)S(1)} %get-tuple-element.19), channel_id=1, source_target_pairs={{0,16},{1,17},{2,18},{3,19},{4,6},{5,7},{6,4},{7,5},{8,24},{9,25},... | collective-permute-start | bytes 196616 | tf_op jit(solution)/shard_map/ppermute | solution.py:154
  19.8 4.3 %collective-permute-start.8 = (bf16[256,128]{1,0:T(8,128)(2,1)S(1)}, bf16[256,128]{1,0:T(8,128)(2,1)S(1)}, u32[]{:S(2)}, u32[]{:S(2)}) collective-permute-start(bf16[256,128]{1,0:T(8,128)(2,1)S(1)} %get-tuple-element.20), channel_id=1, source_target_pairs={{0,8},{1,9},{2,10},{3,11},{4,5},{5,4},{6,7},{7,6},{8,0},{9,1},{10,... | collective-permute-start | bytes 196616 | tf_op jit(solution)/shard_map/ppermute | solution.py:154
  24.1 1.3 %collective-permute-start.9 = (f32[128,128]{1,0:T(8,128)S(1)}, f32[128,128]{1,0:T(8,128)S(1)}, u32[]{:S(2)}, u32[]{:S(2)}) collective-permute-start(f32[128,128]{1,0:T(8,128)S(1)} %get-tuple-element.22), channel_id=1, source_target_pairs={{0,4},{1,5},{2,6},{3,7},{4,0},{5,1},{6,2},{7,3},{8,12},{9,13},{10,... | collective-permute-start | bytes 196616 | tf_op jit(solution)/shard_map/ppermute | solution.py:154

commit v2 on v1

v2 whole, which is shorter than its diff:
```python
import jax
import jax.numpy as jnp
from jax import lax
from jax.experimental import pallas as pl
from jax.experimental.pallas import tpu as pltpu
from jax.sharding import PartitionSpec as P


F32, BF16 = jnp.float32, jnp.bfloat16
AXES = ("row", "col")
VMEM = pl.BlockSpec(memory_space=pltpu.VMEM)
OVER_LAST, OVER_FIRST, PLAIN = ((1,), (1,)), ((0,), (0,)), ((1,), (0,))


def partner(i, distance, n):
    return i ^ distance if n & (n - 1) == 0 else (i + distance) % n


def origin(i, distance, n):
    return i ^ distance if n & (n - 1) == 0 else lax.rem(i + n - distance, n)


def dot(a, b, over):
    return lax.dot_general(a, b, (over, ((), ())), preferred_element_type=F32)


def augmented(raw, inv, first):
    s = (raw.astype(F32) * inv).astype(BF16)
    wide = s.astype(F32)
    rest = -0.5 * jnp.sum(wide * wide, axis=1, keepdims=True)
    lane = lax.broadcasted_iota(jnp.int32, s.shape, 1)
    tail = jnp.zeros(s.shape, F32)
    for n in range(3):
        piece = rest.astype(BF16).astype(F32)
        rest = rest - piece
        tail = jnp.where(lane == (n if first else n + 3), piece, tail)
        tail = jnp.where(lane == (n + 3 if first else n), 1.0, tail)
    return jnp.concatenate([s, tail.astype(BF16)], 1)


def relayout(wide, deep, own, other, own_out, other_out, spare):
    width = own.shape[1]
    at = 0
    for ref, out in ((own, own_out), (other, other_out)):
        for start in range(0, out.shape[0], deep):
            spare[at] = ref[start * wide : (start + deep) * wide, :].astype(F32)
            for a in range(wide):
                rows = spare[at, pl.ds(a, deep, stride=wide), :]
                out[start : start + deep, a * width : (a + 1) * width] = rows
            at = 1 - at


class Layout:
    def __init__(self, lines, planes, pts, width):
        self.lines, self.planes, self.pts, self.width = lines, planes, pts, width
        self.steps = max(lines, planes) - 1
        self.chip = 2 * pts

    def here(self):
        row = lax.axis_index("row")
        return lax.axis_index("col"), lax.div(row, 2), lax.rem(row, 2)

    def rows(self, k, n=1):
        return pl.ds(k * self.chip, n * self.chip)

    def blocks(self, side, lo, hi):
        n = (self.planes, self.lines)[side]
        return [k for k in range(lo, hi) if k == 0 or self.steps + 1 - k < n]

    def groups(self, side, lo, hi):
        have = self.blocks(side, lo, hi)
        return [have[i : i + 3] for i in range(0, len(have), 3)]

    def piece(self, tiles, line, plane):
        at = pl.ds(pl.multiple_of(line * self.pts, self.pts), self.pts)
        cols = pl.ds(pl.multiple_of(plane * self.chip, self.chip), self.chip)
        return jnp.concatenate([tile[at, cols] for tile in tiles], 0)

    def term(self, core, tiles, mine, at, theirs, theirs_at):
        side = jnp.concatenate([theirs[:, : self.width], jnp.ones((self.chip, self.width), BF16)], 1)
        if core:
            e = jnp.exp(dot(mine, theirs, OVER_LAST))
            a = jnp.concatenate([self.piece(tiles, k, theirs_at) for k in at], 0)
            w = (a * e).astype(BF16)
            return dot(w, side, PLAIN)
        e = jnp.exp(dot(theirs, mine, OVER_LAST))
        a = jnp.concatenate([self.piece(tiles, theirs_at, k) for k in at], 1)
        w = (a * e).astype(BF16)
        return dot(w, side, OVER_FIRST)

    def on_each_core(self, body):
        line, plane, core = self.here()
        for c in (0, 1):

            def chip_of(side, k, line=line, plane=plane):
                here, n = ((plane, self.planes), (line, self.lines))[side]
                return origin(here, self.steps + 1 - k, n) if k else here

            @pl.when(core == c)
            def _(c=c, chip_of=chip_of):
                body(c, chip_of)

    def add(self, core, chip_of, tiles, mine, ks, theirs, j):
        return self.term(
            core, tiles, mine, [chip_of(core, k) for k in ks], theirs, chip_of(1 - core, j)
        )

    def early(self, chip, inv, near, a_own, a_other, mine, theirs, part):
        def body(core, chip_of):
            tiles = (a_other, a_own) if core else (a_own, a_other)
            side = augmented(chip[...], inv[...], not core)
            theirs[...] = side
            for k in self.blocks(core, 0, 2):
                block = augmented(near[...] if k else chip[...], inv[...], bool(core))
                mine[self.rows(k), :] = block
                part[self.rows(k), :] = self.add(core, chip_of, tiles, block, [k], side, 0)

        self.on_each_core(body)

    def middle(self, inv, near, far, mine0, theirs0, part0, a_own, a_other, mine, first, part):
        def body(core, chip_of):
            tiles = (a_other, a_own) if core else (a_own, a_other)
            sides = [(0, theirs0[...])]
            for j in self.blocks(1 - core, 1, 2):
                sides.append((j, augmented(far[...], inv[...], not core)))
            for ks in self.groups(core, 2, self.steps + 1):
                rows = self.rows(ks[0] - 2, len(ks))
                block = augmented(near[rows, :], inv[...], bool(core))
                mine[rows, :] = block
                total = self.add(core, chip_of, tiles, block, ks, sides[0][1], 0)
                for j, side in sides[1:]:
                    total += self.add(core, chip_of, tiles, block, ks, side, j)
                part[rows, :] = total
            ks = self.blocks(core, 0, 2)
            rows = self.rows(0, len(ks))
            total = part0[rows, :]
            for j, side in sides[1:]:
                total += self.add(core, chip_of, tiles, mine0[rows, :], ks, side, j)
            first[rows, :] = total

        self.on_each_core(body)

    def closed(self, block, total):
        return total[:, self.width :] * block[:, : self.width].astype(F32) - total[:, : self.width]

    def send(self, inv, far, mine0, mine, first, part, a_own, a_other, theirs, *outs):
        def body(core, chip_of):
            tiles = (a_other, a_own) if core else (a_own, a_other)
            have = self.blocks(1 - core, 2, self.steps + 1)
            few = len(have) <= 3
            sides = {}
            for j in have:
                sides[j] = augmented(far[self.rows(j - 2), :], inv[...], not core)
                theirs[self.rows(j - 2), :] = sides[j]
            for k in range(1, self.steps + 1):
                if k not in self.blocks(core, 1, self.steps + 1):
                    outs[k - 1][...] = jnp.zeros(outs[k - 1].shape, outs[k - 1].dtype)
            for ks in self.groups(core, 1, self.steps + 1):
                parts = [(mine0, first, k) if k == 1 else (mine, part, k - 2) for k in ks]
                block = jnp.concatenate([m[self.rows(at), :] for m, _, at in parts], 0)
                total = jnp.concatenate([p[self.rows(at), :] for _, p, at in parts], 0)
                if few:
                    for j in have:
                        total += self.add(core, chip_of, tiles, block, ks, sides[j], j)
                else:
                    total = self.rest(core, chip_of, tiles, block, ks, theirs, have, total)
                value = self.closed(block, total)
                for n, k in enumerate(ks):
                    out = outs[k - 1]
                    out[...] = value[n * self.chip : (n + 1) * self.chip].astype(out.dtype)

        self.on_each_core(body)

    def rest(self, core, chip_of, tiles, block, ks, theirs, have, total):
        def step(j, total):
            rows = pl.ds(pl.multiple_of((j - 2) * self.chip, self.chip), self.chip)
            side = theirs[rows, :]
            line, plane, _ = self.here()
            here, n = (plane, self.planes) if core else (line, self.lines)
            from_at = origin(here, self.steps + 1 - j, n)
            at = [chip_of(core, k) for k in ks]
            return total + self.term(core, tiles, block, at, side, from_at)

        return lax.fori_loop(have[0], have[-1] + 1, step, total)

    def keep(self, mine0, first, theirs, a_own, a_other, out):
        def body(core, chip_of):
            tiles = (a_other, a_own) if core else (a_own, a_other)
            block, total = mine0[self.rows(0), :], first[self.rows(0), :]
            have = self.blocks(1 - core, 2, self.steps + 1)
            if len(have) <= 3:
                for j in have:
                    total += self.add(core, chip_of, tiles, block, [0], theirs[self.rows(j - 2), :], j)
            else:
                total = self.rest(core, chip_of, tiles, block, [0], theirs, have, total)
            out[...] = self.closed(block, total)

        self.on_each_core(body)

    def total(self, *refs):
        terms, (keep, send) = refs[:-2], refs[-2:]
        core = self.here()[2]
        mine = pl.ds(pl.multiple_of(core * self.pts, self.pts), self.pts)
        other = pl.ds(pl.multiple_of((1 - core) * self.pts, self.pts), self.pts)
        for ref, rows in ((keep, mine), (send, other)):
            acc = terms[0][rows, :].astype(F32)
            for term in terms[1:]:
                acc += term[rows, :].astype(F32)
            ref[...] = acc


def solution(mesh):
    rows, lines = mesh.shape["row"], mesh.shape["col"]
    planes = rows // 2
    steps = max(lines, planes) - 1

    def permute(value, target):
        pairs = []
        for r in range(rows):
            for c in range(lines):
                tr, tc = target(r, c)
                pairs.append((r * lines + c, tr * lines + tc))
        return lax.ppermute(value, AXES, pairs)

    def swap(value):
        return permute(value, lambda r, c: (r ^ 1, c))

    def exchange(value, k):
        distance = steps + 1 - k

        def target(r, c):
            if r % 2:
                return r, partner(c, (distance - 1) % (lines - 1) + 1, lines)
            return 2 * partner(r // 2, (distance - 1) % (planes - 1) + 1, planes), c

        return permute(value, target)

    def local_part(points, abar, inv_scale):
        pts, width = points.shape
        lay = Layout(lines, planes, pts, width)
        chip_rows = lay.chip
        core = lax.axis_index("row") % 2
        inv = inv_scale[None, :]
        grant = pltpu.CompilerParams(vmem_limit_bytes=(6 + steps) * 2**20)

        def call(body, outs, *args):
            return pl.pallas_call(
                body,
                out_shape=[jax.ShapeDtypeStruct(s, t) for s, t in outs],
                in_specs=[VMEM] * len(args),
                out_specs=[VMEM] * len(outs),
                compiler_params=grant,
            )(*args)

        other = swap(points)
        abar_other = swap(abar)
        chip = lax.dynamic_update_slice(
            jnp.zeros((chip_rows, width), points.dtype), points, (core * pts, 0)
        )
        chip = lax.dynamic_update_slice(chip, other, ((1 - core) * pts, 0))
        near = []
        for k in range(1, steps + 1):
            near.append(exchange(chip, k))
        count, wide = abar.shape[0], abar.shape[1] * abar.shape[2]
        cells = [a.reshape(count * wide, abar.shape[3]) for a in (abar, abar_other)]
        if count <= 8 * pts:
            deep = 128
            tiles = pl.pallas_call(
                lambda *refs: relayout(wide, deep, *refs),
                out_shape=[jax.ShapeDtypeStruct((count, wide * width), F32)] * 2,
                in_specs=[VMEM] * 2,
                out_specs=[VMEM] * 2,
                scratch_shapes=[pltpu.VMEM((2, deep * wide, width), F32)],
                compiler_params=grant,
                name="relayout",
            )(*cells)
        else:
            tiles = [a.reshape(count, wide * width).astype(F32) for a in cells]
        far1 = swap(near[0])
        after = jnp.concatenate(near[1:], 0)
        far2 = swap(after)
        deep = 2 * width
        mine0, theirs0, part0 = call(
            lay.early,
            [((2 * chip_rows, deep), BF16), ((chip_rows, deep), BF16), ((2 * chip_rows, deep), F32)],
            chip,
            inv,
            near[0],
            *tiles,
        )
        rest_rows = (steps - 1) * chip_rows
        mine, first, part = call(
            lay.middle,
            [
                ((rest_rows, deep), BF16),
                ((2 * chip_rows, deep), F32),
                ((rest_rows, deep), F32),
            ],
            inv,
            after,
            far1,
            mine0,
            theirs0,
            part0,
            *tiles,
        )
        theirs, *outs = call(
            lay.send,
            [((rest_rows, deep), BF16)] + [((chip_rows, width), BF16)] * steps,
            inv,
            far2,
            mine0,
            mine,
            first,
            part,
            *tiles,
        )
        got = []
        for k in range(1, steps + 1):
            got.append(exchange(outs[k - 1], k))
        (out,) = call(lay.keep, [((chip_rows, width), F32)], mine0, first, theirs, *tiles)
        keep, send = call(lay.total, [((pts, width), F32)] * 2, out, *got)
        return -(keep + swap(send)) * inv

    placed = (P(("row", "col"), None), P("row", None, "col", None), P())
    return jax.shard_map(
        local_part, mesh=mesh, in_specs=placed, out_specs=P(("row", "col"), None), check_vma=False
    )
```

time: 26.2 us -> 26.3 us (level)
  Pallas kernels: 3.45 us -> 4.52 us
  local copies, waits for them, and re-layouts: 2.94 us -> 2.04 us
  waiting for transfers between devices: 10 us -> 9.37 us
  starting transfers between devices: 8.87 us -> 9.42 us
    pallas_call x0 -> x1, Pallas kernels: none -> 0.99 us  [local_part(): pl.pallas_call(lambda *refs: relayout(wide, deep, *refs), out_shape=[jax....]
    unnamed x6 -> x5, local copies, waits for them, and re-layouts: 2.14 us -> 1.23 us
    ppermute x10 -> x11, waiting for transfers between devices: 10 us -> 9.37 us  [permute(): return lax.ppermute(value, AXES, pairs)]
    ppermute x10 -> x11, starting transfers between devices: 8.87 us -> 9.42 us  [permute(): return lax.ppermute(value, AXES, pairs)]
    pallas_call x4 -> x5, Pallas kernels: 3.45 us -> 3.53 us  [call(): pl.pallas_call(body, out_shape=[jax.ShapeDtypeStruct(s, t) for s, t in ou...]
  transfers between devices with their start and end apart: 10 -> 11, of which waited for: 7 -> 7; matrix products, arithmetic and copies ran while one was open for 10% -> 3% of each run, Pallas kernels for 7% -> 14%
where the time goes in v2:
time: 26.3 us; the launch traced here: 26.1 us
  starting transfers between devices  9.42 us (36%)
  waiting for transfers between devices  9.37 us (36%)
  Pallas kernels  4.52 us (17%)
  local copies, waits for them, and re-layouts  2.04 us (8%)
  other arithmetic  0.64 us (2%)
    ppermute x11, starting transfers between devices, permute(): return lax.ppermute(value, AXES, pairs)  9.42 us
    ppermute x11, waiting for transfers between devices, permute(): return lax.ppermute(value, AXES, pairs)  9.37 us
    pallas_call x5, Pallas kernels, call(): pl.pallas_call(body, out_shape=[jax.ShapeDtypeStruct(s, t) for s, t in ou...  3.53 us
    unnamed x5, local copies, waits for them, and re-layouts  1.23 us
    pallas_call x1, Pallas kernels, local_part(): pl.pallas_call(lambda *refs: relayout(wide, deep, *refs), out_shape=[jax....  0.99 us
    dynamic_update_slice x1, local copies, waits for them, and re-layouts, local_part(): lax.dynamic_update_slice(jnp.zeros((chip_rows, width), points.dtype), poi...  0.77 us
    mul x1, other arithmetic, local_part(): return -(keep + swap(send)) * inv  0.64 us
  transfers between devices with their start and end apart: 11, of which 7 were waited for; matrix products, arithmetic and copies ran while one was open for 3% of the time, Pallas kernels for 14%

profile of v2, /device:TPU:0, one launch (start us, length us, event | category | flops | bytes accessed | tf_op | source)
XLA Modules:
  0.0 26.1 jit_solution(6258368588823891944)
XLA Ops:
  0.0 0.0 copy-start.1
  0.0 0.5 %collective-permute-start.2 = (bf16[512,8,1,128]{3,1,2,0:T(8,128)(2,1)}, bf16[512,8,1,128]{3,1,2,0:T(8,128)(2,1)S(1)}, u32[]{:S(2)}, u32[]{:S(2)}) collective-permute-start(bf16[512,8,1,128]{3,1,2,0:T(8,128)(2,1)} %param.4), channel_id=1, source_target_pairs={{0,4},{1,5},{2,6},{3,7},{4,0},{5,1},{6,2},{7,3},{8,12},{9,13},{10,... | collective-permute-start | bytes 3145736 | tf_op jit(solution)/shard_map/ppermute | solution.py:223
  0.5 0.1 collective-permute-start
  0.6 0.8 %constant_dynamic-update-slice_fusion.3 = bf16[256,128]{1,0:T(8,128)(2,1)S(1)} fusion(bf16[256,128]{1,0:T(8,128)(2,1)S(1)} %broadcast_in_dim.6, bf16[128,128]{1,0:T(8,128)(2,1)} %param.3, s32[]{:T(128)S(6)} %select_n.14), kind=kLoop, calls=%fused_computation.4 | loop fusion | bytes 65540 | tf_op jit(solution)/shard_map/dynamic_update_slice | solution.py:257
  1.3 1.7 %collective-permute-done = bf16[128,128]{1,0:T(8,128)(2,1)S(1)} collective-permute-done((bf16[128,128]{1,0:T(8,128)(2,1)}, bf16[128,128]{1,0:T(8,128)(2,1)S(1)}, u32[]{:S(2)}, u32[]{:S(2)}) %collective-permute-start) | collective-permute-done | bytes 32800 | tf_op jit(solution)/shard_map/ppermute | solution.py:223
  3.0 2.9 %collective-permute-start.3 = (bf16[256,128]{1,0:T(8,128)(2,1)S(1)}, bf16[256,128]{1,0:T(8,128)(2,1)S(1)}, u32[]{:S(2)}, u32[]{:S(2)}) collective-permute-start(bf16[256,128]{1,0:T(8,128)(2,1)S(1)} %constant_dynamic-update-slice_fusion.2.chip), channel_id=1, source_target_pairs={{0,16},{1,17},{2,18},{3,19},{4,6},{5,7},{6,4},{7,5},{8,24},{9,25},... | collective-permute-start | bytes 196616 | tf_op jit(solution)/shard_map/ppermute | solution.py:223
  5.9 1.4 %collective-permute-start.1 = (bf16[256,128]{1,0:T(8,128)(2,1)S(1)}, bf16[256,128]{1,0:T(8,128)(2,1)S(1)}, u32[]{:S(2)}, u32[]{:S(2)}) collective-permute-start(bf16[256,128]{1,0:T(8,128)(2,1)S(1)} %constant_dynamic-update-slice_fusion.2.chip), channel_id=1, source_target_pairs={{0,24},{1,25},{2,26},{3,27},{4,7},{5,6},{6,5},{7,4},{8,16},{9,17},... | collective-permute-start | bytes 196616 | tf_op jit(solution)/shard_map/ppermute | solution.py:223
  7.4 0.1 collective-permute-start.4
  7.5 0.7 %collective-permute-done.3 = bf16[256,128]{1,0:T(8,128)(2,1)S(1)} collective-permute-done((bf16[256,128]{1,0:T(8,128)(2,1)S(1)}, bf16[256,128]{1,0:T(8,128)(2,1)S(1)}, u32[]{:S(2)}, u32[]{:S(2)}) %collective-permute-start.3) | collective-permute-done | bytes 65568 | tf_op jit(solution)/shard_map/ppermute | solution.py:223
  8.2 3.5 %collective-permute-done.4 = bf16[256,128]{1,0:T(8,128)(2,1)S(1)} collective-permute-done((bf16[256,128]{1,0:T(8,128)(2,1)S(1)}, bf16[256,128]{1,0:T(8,128)(2,1)S(1)}, u32[]{:S(2)}, u32[]{:S(2)}) %collective-permute-start.4) | collective-permute-done | bytes 65568 | tf_op jit(solution)/shard_map/ppermute | solution.py:223
  11.6 0.1 collective-permute-start.6
  11.7 0.0 collective-permute-done.1.near
  11.7 0.5 %collective-permute-start.5 = (bf16[256,128]{1,0:T(8,128)(2,1)S(1)}, bf16[256,128]{1,0:T(8,128)(2,1)S(1)}, u32[]{:S(2)}, u32[]{:S(2)}) collective-permute-start(bf16[256,128]{1,0:T(8,128)(2,1)S(1)} %collective-permute-done.1.near), channel_id=1, source_target_pairs={{0,4},{1,5},{2,6},{3,7},{4,0},{5,1},{6,2},{7,3},{8,12},{9,13},{10,... | collective-permute-start | bytes 196616 | tf_op jit(solution)/shard_map/ppermute | solution.py:223
  12.2 0.0 collective-permute-done.2
  12.2 0.0 copy-start
  12.2 1.2 %copy-done = bf16[512,8,1,128]{3,1,2,0:T(8,128)(2,1)S(1)} copy-done((bf16[512,8,1,128]{3,1,2,0:T(8,128)(2,1)S(1)}, bf16[512,8,1,128]{3,1,2,0:T(8,128)(2,1)}, u32[]{:S(2)}) %copy-start) | copy-done | bytes 1048600
  13.4 1.0 %relayout.1 = (f32[512,1024]{1,0:T(8,128)S(1)}, f32[512,1024]{1,0:T(8,128)S(1)}) custom-call(bf16[4096,128]{1,0:T(8,128)(2,1)S(1)} %bitcast.3, bf16[4096,128]{1,0:T(8,128)(2,1)S(1)} %bitcast.4), custom_call_target="tpu_custom_call" | custom-call | tf_op jit(solution)/shard_map/relayout/pallas_call | solution.py:268
  14.4 0.0 copy-done.1
  14.5 0.9 %shard_map.37 = (bf16[512,256]{1,0:T(8,128)(2,1)S(1)}, bf16[256,256]{1,0:T(8,128)(2,1)S(1)}, f32[512,256]{1,0:T(8,128)S(1)}) custom-call(bf16[256,128]{1,0:T(8,128)(2,1)S(1)} %constant_dynamic-update-slice_fusion.2.chip, f32[1,128]{1,0:T(1,128)S(1)} %bitcast.5, bf16[256,128]{1,0:T(8,128)(2,1)S(1)} %collective-permute-done.1.near, ...), custom_call_target="tpu_custom_call" | custom-call | tf_op jit(solution)/shard_map/pallas_call | solution.py:247
  15.4 0.0 collective-permute-done.5.far
  15.4 0.9 %shard_map.38 = (bf16[512,256]{1,0:T(8,128)(2,1)S(1)}, f32[512,256]{1,0:T(8,128)S(1)}, f32[512,256]{1,0:T(8,128)S(1)}) custom-call(f32[1,128]{1,0:T(1,128)S(1)} %bitcast.6, bf16[512,128]{1,0:T(8,128)(2,1)S(1)} %constant_dynamic-update-slice_fusion.near, bf16[256,128]{1,0:T(8,128)(2,1)S(1)} %collective-permute-done.5.far, ...), custom_call_target="tpu_custom_call" | custom-call | tf_op jit(solution)/shard_map/pallas_call | solution.py:247
  16.3 0.0 collective-permute-done.6.far
  16.3 0.9 %shard_map.39 = (bf16[512,256]{1,0:T(8,128)(2,1)S(1)}, bf16[256,128]{1,0:T(8,128)(2,1)S(1)}, bf16[256,128]{1,0:T(8,128)(2,1)S(1)}, bf16[256,128]{1,0:T(8,128)(2,1)S(1)}) custom-call(f32[1,128]{1,0:T(1,128)S(1)} %bitcast.7, bf16[512,128]{1,0:T(8,128)(2,1)S(1)} %collective-permute-done.6.far, bf16[512,256]{1,0:T(8,128)(2,1)S(1)} %get-tuple-element.21.mine0, ...), custom_call_target="tpu_custom_call" | custom-call | tf_op jit(solution)/shard_map/pallas_call | solution.py:247
  17.2 2.1 %collective-permute-start.7 = (bf16[256,128]{1,0:T(8,128)(2,1)S(1)}, bf16[256,128]{1,0:T(8,128)(2,1)S(1)}, u32[]{:S(2)}, u32[]{:S(2)}) collective-permute-start(bf16[256,128]{1,0:T(8,128)(2,1)S(1)} %get-tuple-element.28), channel_id=1, source_target_pairs={{0,24},{1,25},{2,26},{3,27},{4,7},{5,6},{6,5},{7,4},{8,16},{9,17},... | collective-permute-start | bytes 196616 | tf_op jit(solution)/shard_map/ppermute | solution.py:223
  19.3 0.5 %collective-permute-start.8 = (bf16[256,128]{1,0:T(8,128)(2,1)S(1)}, bf16[256,128]{1,0:T(8,128)(2,1)S(1)}, u32[]{:S(2)}, u32[]{:S(2)}) collective-permute-start(bf16[256,128]{1,0:T(8,128)(2,1)S(1)} %get-tuple-element.29), channel_id=1, source_target_pairs={{0,16},{1,17},{2,18},{3,19},{4,6},{5,7},{6,4},{7,5},{8,24},{9,25},... | collective-permute-start | bytes 196616 | tf_op jit(solution)/shard_map/ppermute | solution.py:223
  19.8 1.0 %collective-permute-start.9 = (bf16[256,128]{1,0:T(8,128)(2,1)S(1)}, bf16[256,128]{1,0:T(8,128)(2,1)S(1)}, u32[]{:S(2)}, u32[]{:S(2)}) collective-permute-start(bf16[256,128]{1,0:T(8,128)(2,1)S(1)} %get-tuple-element.30), channel_id=1, source_target_pairs={{0,8},{1,9},{2,10},{3,11},{4,5},{5,4},{6,7},{7,6},{8,0},{9,1},{10,... | collective-permute-start | bytes 196616 | tf_op jit(solution)/shard_map/ppermute | solution.py:223
  20.8 0.8 %shard_map.40.refs_0_ = f32[256,128]{1,0:T(8,128)S(1)} custom-call(bf16[512,256]{1,0:T(8,128)(2,1)S(1)} %get-tuple-element.21.mine0, f32[512,256]{1,0:T(8,128)S(1)} %get-tuple-element.24.first, bf16[512,256]{1,0:T(8,128)(2,1)S(1)} %get-tuple-element.27.theirs, f32[512,1024]{1,0:T(8,128)S(1)} %get-tuple-element.19.a_own, ...), custom_call_target="tpu_custom_call" | custom-call | tf_op jit(solution)/shard_map/pallas_call | solution.py:247
  21.6 0.9 %collective-permute-done.7.refs_1_ = bf16[256,128]{1,0:T(8,128)(2,1)S(1)} collective-permute-done((bf16[256,128]{1,0:T(8,128)(2,1)S(1)}, bf16[256,128]{1,0:T(8,128)(2,1)S(1)}, u32[]{:S(2)}, u32[]{:S(2)}) %collective-permute-start.7) | collective-permute-done | bytes 65568 | tf_op jit(solution)/shard_map/ppermute | solution.py:223
  22.5 1.1 %collective-permute-done.8.refs_2_ = bf16[256,128]{1,0:T(8,128)(2,1)S(1)} collective-permute-done((bf16[256,128]{1,0:T(8,128)(2,1)S(1)}, bf16[256,128]{1,0:T(8,128)(2,1)S(1)}, u32[]{:S(2)}, u32[]{:S(2)}) %collective-permute-start.8) | collective-permute-done | bytes 65568 | tf_op jit(solution)/shard_map/ppermute | solution.py:223
  23.6 0.5 %collective-permute-done.9.refs_3_ = bf16[256,128]{1,0:T(8,128)(2,1)S(1)} collective-permute-done((bf16[256,128]{1,0:T(8,128)(2,1)S(1)}, bf16[256,128]{1,0:T(8,128)(2,1)S(1)}, u32[]{:S(2)}, u32[]{:S(2)}) %collective-permute-start.9) | collective-permute-done | bytes 65568 | tf_op jit(solution)/shard_map/ppermute | solution.py:223
  24.1 0.3 %collective-permute-start.10 = (f32[128,128]{1,0:T(8,128)S(1)}, f32[128,128]{1,0:T(8,128)S(1)}, u32[]{:S(2)}, u32[]{:S(2)}) collective-permute-start(f32[128,128]{1,0:T(8,128)S(1)} %get-tuple-element.32), channel_id=1, source_target_pairs={{0,4},{1,5},{2,6},{3,7},{4,0},{5,1},{6,2},{7,3},{8,12},{9,13},{10,... | collective-permute-start | bytes 196616 | tf_op jit(solution)/shard_map/ppermute | solution.py:223
  24.5 1.0 %collective-permute-done.10 = f32[128,128]{1,0:T(8,128)S(1)} collective-permute-done((f32[128,128]{1,0:T(8,128)S(1)}, f32[128,128]{1,0:T(8,128)S(1)}, u32[]{:S(2)}, u32[]{:S(2)}) %collective-permute-start.10) | collective-permute-done | bytes 65568 | tf_op jit(solution)/shard_map/ppermute | solution.py:223
  25.4 0.6 %negate_multiply_fusion = f32[128,128]{1,0:T(8,128)} fusion(f32[128,128]{1,0:T(8,128)S(1)} %get-tuple-element.31, f32[128,128]{1,0:T(8,128)S(1)} %collective-permute-done.10, f32[128]{0:T(128)S(1)} %copy-done.1), kind=kLoop, calls=%fused_computation | loop fusion | flops 49152 | bytes 197120 | tf_op jit(solution)/shard_map/mul | solution.py:323
  (5 shorter events, 0.1 us)
Async XLA Ops:
  0.0 14.4 %copy-start.1 = (f32[128]{0:T(128)S(1)}, f32[128]{0:T(128)}, u32[]{:S(2)}) copy-start(f32[128]{0:T(128)} %param.5) | copy-start | bytes 1540
  0.0 12.2 %collective-permute-start.2 = (bf16[512,8,1,128]{3,1,2,0:T(8,128)(2,1)}, bf16[512,8,1,128]{3,1,2,0:T(8,128)(2,1)S(1)}, u32[]{:S(2)}, u32[]{:S(2)}) collective-permute-start(bf16[512,8,1,128]{3,1,2,0:T(8,128)(2,1)} %param.4), channel_id=1, source_target_pairs={{0,4},{1,5},{2,6},{3,7},{4,0},{5,1},{6,2},{7,3},{8,12},{9,13},{10,... | collective-permute-start | bytes 3145736 | tf_op jit(solution)/shard_map/ppermute | solution.py:223
  0.5 2.5 %collective-permute-start = (bf16[128,128]{1,0:T(8,128)(2,1)}, bf16[128,128]{1,0:T(8,128)(2,1)S(1)}, u32[]{:S(2)}, u32[]{:S(2)}) collective-permute-start(bf16[128,128]{1,0:T(8,128)(2,1)} %param.3), channel_id=1, source_target_pairs={{0,4},{1,5},{2,6},{3,7},{4,0},{5,1},{6,2},{7,3},{8,12},{9,13},{10,... | collective-permute-start | bytes 98312 | tf_op jit(solution)/shard_map/ppermute | solution.py:223
  3.0 5.1 %collective-permute-start.3 = (bf16[256,128]{1,0:T(8,128)(2,1)S(1)}, bf16[256,128]{1,0:T(8,128)(2,1)S(1)}, u32[]{:S(2)}, u32[]{:S(2)}) collective-permute-start(bf16[256,128]{1,0:T(8,128)(2,1)S(1)} %constant_dynamic-update-slice_fusion.2.chip), channel_id=1, source_target_pairs={{0,16},{1,17},{2,18},{3,19},{4,6},{5,7},{6,4},{7,5},{8,24},{9,25},... | collective-permute-start | bytes 196616 | tf_op jit(solution)/shard_map/ppermute | solution.py:223
  5.9 5.8 %collective-permute-start.1 = (bf16[256,128]{1,0:T(8,128)(2,1)S(1)}, bf16[256,128]{1,0:T(8,128)(2,1)S(1)}, u32[]{:S(2)}, u32[]{:S(2)}) collective-permute-start(bf16[256,128]{1,0:T(8,128)(2,1)S(1)} %constant_dynamic-update-slice_fusion.2.chip), channel_id=1, source_target_pairs={{0,24},{1,25},{2,26},{3,27},{4,7},{5,6},{6,5},{7,4},{8,16},{9,17},... | collective-permute-start | bytes 196616 | tf_op jit(solution)/shard_map/ppermute | solution.py:223
  7.4 4.3 %collective-permute-start.4 = (bf16[256,128]{1,0:T(8,128)(2,1)S(1)}, bf16[256,128]{1,0:T(8,128)(2,1)S(1)}, u32[]{:S(2)}, u32[]{:S(2)}) collective-permute-start(bf16[256,128]{1,0:T(8,128)(2,1)S(1)} %constant_dynamic-update-slice_fusion.2.chip), channel_id=1, source_target_pairs={{0,8},{1,9},{2,10},{3,11},{4,5},{5,4},{6,7},{7,6},{8,0},{9,1},{10,... | collective-permute-start | bytes 196616 | tf_op jit(solution)/shard_map/ppermute | solution.py:223
  11.6 4.7 %collective-permute-start.6 = (bf16[512,128]{1,0:T(8,128)(2,1)S(1)}, bf16[512,128]{1,0:T(8,128)(2,1)S(1)}, u32[]{:S(2)}, u32[]{:S(2)}) collective-permute-start(bf16[512,128]{1,0:T(8,128)(2,1)S(1)} %constant_dynamic-update-slice_fusion.near), channel_id=1, source_target_pairs={{0,4},{1,5},{2,6},{3,7},{4,0},{5,1},{6,2},{7,3},{8,12},{9,13},{10,... | collective-permute-start | bytes 393224 | tf_op jit(solution)/shard_map/ppermute | solution.py:223
  11.7 3.6 %collective-permute-start.5 = (bf16[256,128]{1,0:T(8,128)(2,1)S(1)}, bf16[256,128]{1,0:T(8,128)(2,1)S(1)}, u32[]{:S(2)}, u32[]{:S(2)}) collective-permute-start(bf16[256,128]{1,0:T(8,128)(2,1)S(1)} %collective-permute-done.1.near), channel_id=1, source_target_pairs={{0,4},{1,5},{2,6},{3,7},{4,0},{5,1},{6,2},{7,3},{8,12},{9,13},{10,... | collective-permute-start | bytes 196616 | tf_op jit(solution)/shard_map/ppermute | solution.py:223
  12.2 1.2 %copy-start = (bf16[512,8,1,128]{3,1,2,0:T(8,128)(2,1)S(1)}, bf16[512,8,1,128]{3,1,2,0:T(8,128)(2,1)}, u32[]{:S(2)}) copy-start(bf16[512,8,1,128]{3,1,2,0:T(8,128)(2,1)} %param.4) | copy-start | bytes 3145732
  17.2 5.2 %collective-permute-start.7 = (bf16[256,128]{1,0:T(8,128)(2,1)S(1)}, bf16[256,128]{1,0:T(8,128)(2,1)S(1)}, u32[]{:S(2)}, u32[]{:S(2)}) collective-permute-start(bf16[256,128]{1,0:T(8,128)(2,1)S(1)} %get-tuple-element.28), channel_id=1, source_target_pairs={{0,24},{1,25},{2,26},{3,27},{4,7},{5,6},{6,5},{7,4},{8,16},{9,17},... | collective-permute-start | bytes 196616 | tf_op jit(solution)/shard_map/ppermute | solution.py:223
  19.3 4.3 %collective-permute-start.8 = (bf16[256,128]{1,0:T(8,128)(2,1)S(1)}, bf16[256,128]{1,0:T(8,128)(2,1)S(1)}, u32[]{:S(2)}, u32[]{:S(2)}) collective-permute-start(bf16[256,128]{1,0:T(8,128)(2,1)S(1)} %get-tuple-element.29), channel_id=1, source_target_pairs={{0,16},{1,17},{2,18},{3,19},{4,6},{5,7},{6,4},{7,5},{8,24},{9,25},... | collective-permute-start | bytes 196616 | tf_op jit(solution)/shard_map/ppermute | solution.py:223
  19.8 4.3 %collective-permute-start.9 = (bf16[256,128]{1,0:T(8,128)(2,1)S(1)}, bf16[256,128]{1,0:T(8,128)(2,1)S(1)}, u32[]{:S(2)}, u32[]{:S(2)}) collective-permute-start(bf16[256,128]{1,0:T(8,128)(2,1)S(1)} %get-tuple-element.30), channel_id=1, source_target_pairs={{0,8},{1,9},{2,10},{3,11},{4,5},{5,4},{6,7},{7,6},{8,0},{9,1},{10,... | collective-permute-start | bytes 196616 | tf_op jit(solution)/shard_map/ppermute | solution.py:223
  24.1 1.3 %collective-permute-start.10 = (f32[128,128]{1,0:T(8,128)S(1)}, f32[128,128]{1,0:T(8,128)S(1)}, u32[]{:S(2)}, u32[]{:S(2)}) collective-permute-start(f32[128,128]{1,0:T(8,128)S(1)} %get-tuple-element.32), channel_id=1, source_target_pairs={{0,4},{1,5},{2,6},{3,7},{4,0},{5,1},{6,2},{7,3},{8,12},{9,13},{10,... | collective-permute-start | bytes 196616 | tf_op jit(solution)/shard_map/ppermute | solution.py:223

commit v3 on v2

--- a/solution.py
+++ b/solution.py
@@ -29,12 +29,11 @@
     wide = s.astype(F32)
     rest = -0.5 * jnp.sum(wide * wide, axis=1, keepdims=True)
     lane = lax.broadcasted_iota(jnp.int32, s.shape, 1)
-    tail = jnp.zeros(s.shape, F32)
+    at, ones = (0, 3) if first else (3, 0)
+    tail = jnp.where((lane >= ones) & (lane < ones + 3), 1.0, 0.0)
     for n in range(3):
-        piece = rest.astype(BF16).astype(F32)
-        rest = rest - piece
-        tail = jnp.where(lane == (n if first else n + 3), piece, tail)
-        tail = jnp.where(lane == (n + 3 if first else n), 1.0, tail)
+        tail = jnp.where(lane == at + n, rest, tail)
+        rest = rest - rest.astype(BF16).astype(F32)
     return jnp.concatenate([s, tail.astype(BF16)], 1)
 
 
@@ -77,16 +76,22 @@
         return jnp.concatenate([tile[at, cols] for tile in tiles], 0)
 
     def term(self, core, tiles, mine, at, theirs, theirs_at):
-        side = jnp.concatenate([theirs[:, : self.width], jnp.ones((self.chip, self.width), BF16)], 1)
+        if not core and len(at) > 1 and len(theirs_at) > 1:
+            parts = []
+            for n, j in enumerate(theirs_at):
+                rows = theirs[n * self.chip : (n + 1) * self.chip]
+                parts.append(self.term(core, tiles, mine, at, rows, [j]))
+            return sum(parts[1:], parts[0])
+        ones = jnp.ones((theirs.shape[0], self.width), BF16)
+        side = jnp.concatenate([theirs[:, : self.width], ones], 1)
         if core:
             e = jnp.exp(dot(mine, theirs, OVER_LAST))
-            a = jnp.concatenate([self.piece(tiles, k, theirs_at) for k in at], 0)
-            w = (a * e).astype(BF16)
-            return dot(w, side, PLAIN)
-        e = jnp.exp(dot(theirs, mine, OVER_LAST))
-        a = jnp.concatenate([self.piece(tiles, theirs_at, k) for k in at], 1)
-        w = (a * e).astype(BF16)
-        return dot(w, side, OVER_FIRST)
+            rows = [[self.piece(tiles, k, j) for j in theirs_at] for k in at]
+        else:
+            e = jnp.exp(dot(theirs, mine, OVER_LAST))
+            rows = [[self.piece(tiles, j, k) for k in at] for j in theirs_at]
+        a = jnp.concatenate([jnp.concatenate(row, 1) for row in rows], 0)
+        return dot((a * e).astype(BF16), side, PLAIN if core else OVER_FIRST)
 
     def on_each_core(self, body):
         line, plane, core = self.here()
@@ -100,10 +105,9 @@
             def _(c=c, chip_of=chip_of):
                 body(c, chip_of)
 
-    def add(self, core, chip_of, tiles, mine, ks, theirs, j):
-        return self.term(
-            core, tiles, mine, [chip_of(core, k) for k in ks], theirs, chip_of(1 - core, j)
-        )
+    def add(self, core, chip_of, tiles, mine, ks, theirs, js):
+        at, from_at = [chip_of(core, k) for k in ks], [chip_of(1 - core, j) for j in js]
+        return self.term(core, tiles, mine, at, theirs, from_at)
 
     def early(self, chip, inv, near, a_own, a_other, mine, theirs, part):
         def body(core, chip_of):
@@ -113,29 +117,28 @@
             for k in self.blocks(core, 0, 2):
                 block = augmented(near[...] if k else chip[...], inv[...], bool(core))
                 mine[self.rows(k), :] = block
-                part[self.rows(k), :] = self.add(core, chip_of, tiles, block, [k], side, 0)
+                part[self.rows(k), :] = self.add(core, chip_of, tiles, block, [k], side, [0])
 
         self.on_each_core(body)
 
     def middle(self, inv, near, far, mine0, theirs0, part0, a_own, a_other, mine, first, part):
         def body(core, chip_of):
             tiles = (a_other, a_own) if core else (a_own, a_other)
-            sides = [(0, theirs0[...])]
-            for j in self.blocks(1 - core, 1, 2):
-                sides.append((j, augmented(far[...], inv[...], not core)))
+            new = self.blocks(1 - core, 1, 2)
+            sides = theirs0[...]
+            if new:
+                side = augmented(far[...], inv[...], not core)
+                sides = jnp.concatenate([sides, side], 0)
             for ks in self.groups(core, 2, self.steps + 1):
                 rows = self.rows(ks[0] - 2, len(ks))
                 block = augmented(near[rows, :], inv[...], bool(core))
                 mine[rows, :] = block
-                total = self.add(core, chip_of, tiles, block, ks, sides[0][1], 0)
-                for j, side in sides[1:]:
-                    total += self.add(core, chip_of, tiles, block, ks, side, j)
-                part[rows, :] = total
+                part[rows, :] = self.add(core, chip_of, tiles, block, ks, sides, [0] + new)
             ks = self.blocks(core, 0, 2)
             rows = self.rows(0, len(ks))
             total = part0[rows, :]
-            for j, side in sides[1:]:
-                total += self.add(core, chip_of, tiles, mine0[rows, :], ks, side, j)
+            if new:
+                total += self.add(core, chip_of, tiles, mine0[rows, :], ks, side, new)
             first[rows, :] = total
 
         self.on_each_core(body)
@@ -148,10 +151,9 @@
             tiles = (a_other, a_own) if core else (a_own, a_other)
             have = self.blocks(1 - core, 2, self.steps + 1)
             few = len(have) <= 3
-            sides = {}
-            for j in have:
-                sides[j] = augmented(far[self.rows(j - 2), :], inv[...], not core)
-                theirs[self.rows(j - 2), :] = sides[j]
+            given = self.rows(have[0] - 2, len(have))
+            side = augmented(far[given, :], inv[...], not core)
+            theirs[given, :] = side
             for k in range(1, self.steps + 1):
                 if k not in self.blocks(core, 1, self.steps + 1):
                     outs[k - 1][...] = jnp.zeros(outs[k - 1].shape, outs[k - 1].dtype)
@@ -160,8 +162,7 @@
                 block = jnp.concatenate([m[self.rows(at), :] for m, _, at in parts], 0)
                 total = jnp.concatenate([p[self.rows(at), :] for _, p, at in parts], 0)
                 if few:
-                    for j in have:
-                        total += self.add(core, chip_of, tiles, block, ks, sides[j], j)
+                    total += self.add(core, chip_of, tiles, block, ks, side, have)
                 else:
                     total = self.rest(core, chip_of, tiles, block, ks, theirs, have, total)
                 value = self.closed(block, total)
@@ -179,7 +180,7 @@
             here, n = (plane, self.planes) if core else (line, self.lines)
             from_at = origin(here, self.steps + 1 - j, n)
             at = [chip_of(core, k) for k in ks]
-            return total + self.term(core, tiles, block, at, side, from_at)
+            return total + self.term(core, tiles, block, at, side, [from_at])
 
         return lax.fori_loop(have[0], have[-1] + 1, step, total)
 
@@ -189,8 +190,8 @@
             block, total = mine0[self.rows(0), :], first[self.rows(0), :]
             have = self.blocks(1 - core, 2, self.steps + 1)
             if len(have) <= 3:
-                for j in have:
-                    total += self.add(core, chip_of, tiles, block, [0], theirs[self.rows(j - 2), :], j)
+                side = theirs[self.rows(have[0] - 2, len(have)), :]
+                total += self.add(core, chip_of, tiles, block, [0], side, have)
             else:
                 total = self.rest(core, chip_of, tiles, block, [0], theirs, have, total)
             out[...] = self.closed(block, total)
@@ -198,7 +199,7 @@
         self.on_each_core(body)
 
     def total(self, *refs):
-        terms, (keep, send) = refs[:-2], refs[-2:]
+        inv, terms, (keep, send) = refs[0], refs[1:-2], refs[-2:]
         core = self.here()[2]
         mine = pl.ds(pl.multiple_of(core * self.pts, self.pts), self.pts)
         other = pl.ds(pl.multiple_of((1 - core) * self.pts, self.pts), self.pts)
@@ -206,7 +207,7 @@
             acc = terms[0][rows, :].astype(F32)
             for term in terms[1:]:
                 acc += term[rows, :].astype(F32)
-            ref[...] = acc
+            ref[...] = -acc * inv[...]
 
 
 def solution(mesh):
@@ -319,8 +320,8 @@
         for k in range(1, steps + 1):
             got.append(exchange(outs[k - 1], k))
         (out,) = call(lay.keep, [((chip_rows, width), F32)], mine0, first, theirs, *tiles)
-        keep, send = call(lay.total, [((pts, width), F32)] * 2, out, *got)
-        return -(keep + swap(send)) * inv
+        keep, send = call(lay.total, [((pts, width), F32)] * 2, inv, out, *got)
+        return keep + swap(send)
 
     placed = (P(("row", "col"), None), P("row", None, "col", None), P())
     return jax.shard_map(

time: 26.3 us -> 26.1 us (level)
  Pallas kernels: 4.52 us -> 4.17 us
    mul x1 -> x0, other arithmetic: 0.64 us -> none  [local_part(): return -(keep + swap(send)) * inv]
    add x0 -> x1, other arithmetic: none -> 0.64 us  [local_part(): return keep + swap(send)]
    pallas_call x5, Pallas kernels: 3.53 us -> 3.18 us  [call(): pl.pallas_call(body, out_shape=[jax.ShapeDtypeStruct(s, t) for s, t in ou...]
  transfers between devices with their start and end apart: 11 -> 11, of which waited for: 7 -> 7; matrix products, arithmetic and copies ran while one was open for 3% -> 3% of each run, Pallas kernels for 14% -> 13%
where the time goes in v3:
time: 26.1 us; the launch traced here: 25.9 us
  waiting for transfers between devices  9.54 us (37%)
  starting transfers between devices  9.44 us (36%)
  Pallas kernels  4.17 us (16%)
  local copies, waits for them, and re-layouts  2.04 us (8%)
  other arithmetic  0.64 us (2%)
    ppermute x11, waiting for transfers between devices, permute(): return lax.ppermute(value, AXES, pairs)  9.54 us
    ppermute x11, starting transfers between devices, permute(): return lax.ppermute(value, AXES, pairs)  9.44 us
    pallas_call x5, Pallas kernels, call(): pl.pallas_call(body, out_shape=[jax.ShapeDtypeStruct(s, t) for s, t in ou...  3.18 us
    unnamed x5, local copies, waits for them, and re-layouts  1.23 us
    pallas_call x1, Pallas kernels, local_part(): pl.pallas_call(lambda *refs: relayout(wide, deep, *refs), out_shape=[jax....  0.99 us
    dynamic_update_slice x1, local copies, waits for them, and re-layouts, local_part(): lax.dynamic_update_slice(jnp.zeros((chip_rows, width), points.dtype), poi...  0.77 us
    add x1, other arithmetic, local_part(): return keep + swap(send)  0.64 us
  transfers between devices with their start and end apart: 11, of which 7 were waited for; matrix products, arithmetic and copies ran while one was open for 3% of the time, Pallas kernels for 13%

profile of v3, /device:TPU:0, one launch (start us, length us, event | category | flops | bytes accessed | tf_op | source)
XLA Modules:
  0.0 25.9 jit_solution(7076539727854695282)
XLA Ops:
  0.0 0.0 copy-start.1
  0.0 0.5 %collective-permute-start.2 = (bf16[512,8,1,128]{3,1,2,0:T(8,128)(2,1)}, bf16[512,8,1,128]{3,1,2,0:T(8,128)(2,1)S(1)}, u32[]{:S(2)}, u32[]{:S(2)}) collective-permute-start(bf16[512,8,1,128]{3,1,2,0:T(8,128)(2,1)} %param.4), channel_id=1, source_target_pairs={{0,4},{1,5},{2,6},{3,7},{4,0},{5,1},{6,2},{7,3},{8,12},{9,13},{10,... | collective-permute-start | bytes 3145736 | tf_op jit(solution)/shard_map/ppermute | solution.py:224
  0.5 0.1 collective-permute-start
  0.6 0.8 %constant_dynamic-update-slice_fusion.3 = bf16[256,128]{1,0:T(8,128)(2,1)S(1)} fusion(bf16[256,128]{1,0:T(8,128)(2,1)S(1)} %broadcast_in_dim.7, bf16[128,128]{1,0:T(8,128)(2,1)} %param.3, s32[]{:T(128)S(6)} %select_n.14), kind=kLoop, calls=%fused_computation.3 | loop fusion | bytes 65540 | tf_op jit(solution)/shard_map/dynamic_update_slice | solution.py:258
  1.3 1.7 %collective-permute-done = bf16[128,128]{1,0:T(8,128)(2,1)S(1)} collective-permute-done((bf16[128,128]{1,0:T(8,128)(2,1)}, bf16[128,128]{1,0:T(8,128)(2,1)S(1)}, u32[]{:S(2)}, u32[]{:S(2)}) %collective-permute-start) | collective-permute-done | bytes 32800 | tf_op jit(solution)/shard_map/ppermute | solution.py:224
  3.0 2.9 %collective-permute-start.3 = (bf16[256,128]{1,0:T(8,128)(2,1)S(1)}, bf16[256,128]{1,0:T(8,128)(2,1)S(1)}, u32[]{:S(2)}, u32[]{:S(2)}) collective-permute-start(bf16[256,128]{1,0:T(8,128)(2,1)S(1)} %constant_dynamic-update-slice_fusion.2.chip), channel_id=1, source_target_pairs={{0,16},{1,17},{2,18},{3,19},{4,6},{5,7},{6,4},{7,5},{8,24},{9,25},... | collective-permute-start | bytes 196616 | tf_op jit(solution)/shard_map/ppermute | solution.py:224
  5.9 1.4 %collective-permute-start.1 = (bf16[256,128]{1,0:T(8,128)(2,1)S(1)}, bf16[256,128]{1,0:T(8,128)(2,1)S(1)}, u32[]{:S(2)}, u32[]{:S(2)}) collective-permute-start(bf16[256,128]{1,0:T(8,128)(2,1)S(1)} %constant_dynamic-update-slice_fusion.2.chip), channel_id=1, source_target_pairs={{0,24},{1,25},{2,26},{3,27},{4,7},{5,6},{6,5},{7,4},{8,16},{9,17},... | collective-permute-start | bytes 196616 | tf_op jit(solution)/shard_map/ppermute | solution.py:224
  7.4 0.1 collective-permute-start.4
  7.5 0.7 %collective-permute-done.3 = bf16[256,128]{1,0:T(8,128)(2,1)S(1)} collective-permute-done((bf16[256,128]{1,0:T(8,128)(2,1)S(1)}, bf16[256,128]{1,0:T(8,128)(2,1)S(1)}, u32[]{:S(2)}, u32[]{:S(2)}) %collective-permute-start.3) | collective-permute-done | bytes 65568 | tf_op jit(solution)/shard_map/ppermute | solution.py:224
  8.2 3.5 %collective-permute-done.4 = bf16[256,128]{1,0:T(8,128)(2,1)S(1)} collective-permute-done((bf16[256,128]{1,0:T(8,128)(2,1)S(1)}, bf16[256,128]{1,0:T(8,128)(2,1)S(1)}, u32[]{:S(2)}, u32[]{:S(2)}) %collective-permute-start.4) | collective-permute-done | bytes 65568 | tf_op jit(solution)/shard_map/ppermute | solution.py:224
  11.6 0.1 collective-permute-start.6
  11.7 0.0 collective-permute-done.1.near
  11.7 0.5 %collective-permute-start.5 = (bf16[256,128]{1,0:T(8,128)(2,1)S(1)}, bf16[256,128]{1,0:T(8,128)(2,1)S(1)}, u32[]{:S(2)}, u32[]{:S(2)}) collective-permute-start(bf16[256,128]{1,0:T(8,128)(2,1)S(1)} %collective-permute-done.1.near), channel_id=1, source_target_pairs={{0,4},{1,5},{2,6},{3,7},{4,0},{5,1},{6,2},{7,3},{8,12},{9,13},{10,... | collective-permute-start | bytes 196616 | tf_op jit(solution)/shard_map/ppermute | solution.py:224
  12.2 0.0 collective-permute-done.2
  12.2 0.0 copy-start
  12.2 1.2 %copy-done = bf16[512,8,1,128]{3,1,2,0:T(8,128)(2,1)S(1)} copy-done((bf16[512,8,1,128]{3,1,2,0:T(8,128)(2,1)S(1)}, bf16[512,8,1,128]{3,1,2,0:T(8,128)(2,1)}, u32[]{:S(2)}) %copy-start) | copy-done | bytes 1048600
  13.4 1.0 %relayout.1 = (f32[512,1024]{1,0:T(8,128)S(1)}, f32[512,1024]{1,0:T(8,128)S(1)}) custom-call(bf16[4096,128]{1,0:T(8,128)(2,1)S(1)} %bitcast.3, bf16[4096,128]{1,0:T(8,128)(2,1)S(1)} %bitcast.4), custom_call_target="tpu_custom_call" | custom-call | tf_op jit(solution)/shard_map/relayout/pallas_call | solution.py:269
  14.4 0.0 copy-done.1
  14.5 0.9 %shard_map.37 = (bf16[512,256]{1,0:T(8,128)(2,1)S(1)}, bf16[256,256]{1,0:T(8,128)(2,1)S(1)}, f32[512,256]{1,0:T(8,128)S(1)}) custom-call(bf16[256,128]{1,0:T(8,128)(2,1)S(1)} %constant_dynamic-update-slice_fusion.2.chip, f32[1,128]{1,0:T(1,128)S(1)} %bitcast.5, bf16[256,128]{1,0:T(8,128)(2,1)S(1)} %collective-permute-done.1.near, ...), custom_call_target="tpu_custom_call" | custom-call | tf_op jit(solution)/shard_map/pallas_call | solution.py:248
  15.4 0.0 collective-permute-done.5.far
  15.4 0.9 %shard_map.38 = (bf16[512,256]{1,0:T(8,128)(2,1)S(1)}, f32[512,256]{1,0:T(8,128)S(1)}, f32[512,256]{1,0:T(8,128)S(1)}) custom-call(f32[1,128]{1,0:T(1,128)S(1)} %bitcast.6, bf16[512,128]{1,0:T(8,128)(2,1)S(1)} %constant_dynamic-update-slice_fusion.near, bf16[256,128]{1,0:T(8,128)(2,1)S(1)} %collective-permute-done.5.far, ...), custom_call_target="tpu_custom_call" | custom-call | tf_op jit(solution)/shard_map/pallas_call | solution.py:248
  16.3 0.0 collective-permute-done.6.far
  16.3 0.8 %shard_map.39 = (bf16[512,256]{1,0:T(8,128)(2,1)S(1)}, bf16[256,128]{1,0:T(8,128)(2,1)S(1)}, bf16[256,128]{1,0:T(8,128)(2,1)S(1)}, bf16[256,128]{1,0:T(8,128)(2,1)S(1)}) custom-call(f32[1,128]{1,0:T(1,128)S(1)} %bitcast.7, bf16[512,128]{1,0:T(8,128)(2,1)S(1)} %collective-permute-done.6.far, bf16[512,256]{1,0:T(8,128)(2,1)S(1)} %get-tuple-element.21.mine0, ...), custom_call_target="tpu_custom_call" | custom-call | tf_op jit(solution)/shard_map/pallas_call | solution.py:248
  17.1 2.1 %collective-permute-start.7 = (bf16[256,128]{1,0:T(8,128)(2,1)S(1)}, bf16[256,128]{1,0:T(8,128)(2,1)S(1)}, u32[]{:S(2)}, u32[]{:S(2)}) collective-permute-start(bf16[256,128]{1,0:T(8,128)(2,1)S(1)} %get-tuple-element.28), channel_id=1, source_target_pairs={{0,24},{1,25},{2,26},{3,27},{4,7},{5,6},{6,5},{7,4},{8,16},{9,17},... | collective-permute-start | bytes 196616 | tf_op jit(solution)/shard_map/ppermute | solution.py:224
  19.2 0.5 %collective-permute-start.8 = (bf16[256,128]{1,0:T(8,128)(2,1)S(1)}, bf16[256,128]{1,0:T(8,128)(2,1)S(1)}, u32[]{:S(2)}, u32[]{:S(2)}) collective-permute-start(bf16[256,128]{1,0:T(8,128)(2,1)S(1)} %get-tuple-element.29), channel_id=1, source_target_pairs={{0,16},{1,17},{2,18},{3,19},{4,6},{5,7},{6,4},{7,5},{8,24},{9,25},... | collective-permute-start | bytes 196616 | tf_op jit(solution)/shard_map/ppermute | solution.py:224
  19.7 1.0 %collective-permute-start.9 = (bf16[256,128]{1,0:T(8,128)(2,1)S(1)}, bf16[256,128]{1,0:T(8,128)(2,1)S(1)}, u32[]{:S(2)}, u32[]{:S(2)}) collective-permute-start(bf16[256,128]{1,0:T(8,128)(2,1)S(1)} %get-tuple-element.30), channel_id=1, source_target_pairs={{0,8},{1,9},{2,10},{3,11},{4,5},{5,4},{6,7},{7,6},{8,0},{9,1},{10,... | collective-permute-start | bytes 196616 | tf_op jit(solution)/shard_map/ppermute | solution.py:224
  20.6 0.5 %shard_map.40.refs_1_ = f32[256,128]{1,0:T(8,128)S(1)} custom-call(bf16[512,256]{1,0:T(8,128)(2,1)S(1)} %get-tuple-element.21.mine0, f32[512,256]{1,0:T(8,128)S(1)} %get-tuple-element.24.first, bf16[512,256]{1,0:T(8,128)(2,1)S(1)} %get-tuple-element.27.theirs, f32[512,1024]{1,0:T(8,128)S(1)} %get-tuple-element.19.a_own, ...), custom_call_target="tpu_custom_call" | custom-call | tf_op jit(solution)/shard_map/pallas_call | solution.py:248
  21.2 1.1 %collective-permute-done.7.refs_2_ = bf16[256,128]{1,0:T(8,128)(2,1)S(1)} collective-permute-done((bf16[256,128]{1,0:T(8,128)(2,1)S(1)}, bf16[256,128]{1,0:T(8,128)(2,1)S(1)}, u32[]{:S(2)}, u32[]{:S(2)}) %collective-permute-start.7) | collective-permute-done | bytes 65568 | tf_op jit(solution)/shard_map/ppermute | solution.py:224
  22.3 1.1 %collective-permute-done.8.refs_3_ = bf16[256,128]{1,0:T(8,128)(2,1)S(1)} collective-permute-done((bf16[256,128]{1,0:T(8,128)(2,1)S(1)}, bf16[256,128]{1,0:T(8,128)(2,1)S(1)}, u32[]{:S(2)}, u32[]{:S(2)}) %collective-permute-start.8) | collective-permute-done | bytes 65568 | tf_op jit(solution)/shard_map/ppermute | solution.py:224
  23.4 0.5 %collective-permute-done.9.refs_4_ = bf16[256,128]{1,0:T(8,128)(2,1)S(1)} collective-permute-done((bf16[256,128]{1,0:T(8,128)(2,1)S(1)}, bf16[256,128]{1,0:T(8,128)(2,1)S(1)}, u32[]{:S(2)}, u32[]{:S(2)}) %collective-permute-start.9) | collective-permute-done | bytes 65568 | tf_op jit(solution)/shard_map/ppermute | solution.py:224
  24.0 0.4 %collective-permute-start.10 = (f32[128,128]{1,0:T(8,128)S(1)}, f32[128,128]{1,0:T(8,128)S(1)}, u32[]{:S(2)}, u32[]{:S(2)}) collective-permute-start(f32[128,128]{1,0:T(8,128)S(1)} %get-tuple-element.32), channel_id=1, source_target_pairs={{0,4},{1,5},{2,6},{3,7},{4,0},{5,1},{6,2},{7,3},{8,12},{9,13},{10,... | collective-permute-start | bytes 196616 | tf_op jit(solution)/shard_map/ppermute | solution.py:224
  24.3 1.0 %collective-permute-done.10 = f32[128,128]{1,0:T(8,128)S(1)} collective-permute-done((f32[128,128]{1,0:T(8,128)S(1)}, f32[128,128]{1,0:T(8,128)S(1)}, u32[]{:S(2)}, u32[]{:S(2)}) %collective-permute-start.10) | collective-permute-done | bytes 65568 | tf_op jit(solution)/shard_map/ppermute | solution.py:224
  25.3 0.6 %add.16 = f32[128,128]{1,0:T(8,128)} add(f32[128,128]{1,0:T(8,128)S(1)} %get-tuple-element.31, f32[128,128]{1,0:T(8,128)S(1)} %collective-permute-done.10) | non-fusion elementwise | flops 16384 | bytes 196608 | tf_op jit(solution)/shard_map/add | solution.py:324
  (5 shorter events, 0.1 us)
Async XLA Ops:
  0.0 14.4 %copy-start.1 = (f32[128]{0:T(128)S(1)}, f32[128]{0:T(128)}, u32[]{:S(2)}) copy-start(f32[128]{0:T(128)} %param.5) | copy-start | bytes 1540
  0.0 12.2 %collective-permute-start.2 = (bf16[512,8,1,128]{3,1,2,0:T(8,128)(2,1)}, bf16[512,8,1,128]{3,1,2,0:T(8,128)(2,1)S(1)}, u32[]{:S(2)}, u32[]{:S(2)}) collective-permute-start(bf16[512,8,1,128]{3,1,2,0:T(8,128)(2,1)} %param.4), channel_id=1, source_target_pairs={{0,4},{1,5},{2,6},{3,7},{4,0},{5,1},{6,2},{7,3},{8,12},{9,13},{10,... | collective-permute-start | bytes 3145736 | tf_op jit(solution)/shard_map/ppermute | solution.py:224
  0.5 2.5 %collective-permute-start = (bf16[128,128]{1,0:T(8,128)(2,1)}, bf16[128,128]{1,0:T(8,128)(2,1)S(1)}, u32[]{:S(2)}, u32[]{:S(2)}) collective-permute-start(bf16[128,128]{1,0:T(8,128)(2,1)} %param.3), channel_id=1, source_target_pairs={{0,4},{1,5},{2,6},{3,7},{4,0},{5,1},{6,2},{7,3},{8,12},{9,13},{10,... | collective-permute-start | bytes 98312 | tf_op jit(solution)/shard_map/ppermute | solution.py:224
  3.0 5.1 %collective-permute-start.3 = (bf16[256,128]{1,0:T(8,128)(2,1)S(1)}, bf16[256,128]{1,0:T(8,128)(2,1)S(1)}, u32[]{:S(2)}, u32[]{:S(2)}) collective-permute-start(bf16[256,128]{1,0:T(8,128)(2,1)S(1)} %constant_dynamic-update-slice_fusion.2.chip), channel_id=1, source_target_pairs={{0,16},{1,17},{2,18},{3,19},{4,6},{5,7},{6,4},{7,5},{8,24},{9,25},... | collective-permute-start | bytes 196616 | tf_op jit(solution)/shard_map/ppermute | solution.py:224
  5.9 5.8 %collective-permute-start.1 = (bf16[256,128]{1,0:T(8,128)(2,1)S(1)}, bf16[256,128]{1,0:T(8,128)(2,1)S(1)}, u32[]{:S(2)}, u32[]{:S(2)}) collective-permute-start(bf16[256,128]{1,0:T(8,128)(2,1)S(1)} %constant_dynamic-update-slice_fusion.2.chip), channel_id=1, source_target_pairs={{0,24},{1,25},{2,26},{3,27},{4,7},{5,6},{6,5},{7,4},{8,16},{9,17},... | collective-permute-start | bytes 196616 | tf_op jit(solution)/shard_map/ppermute | solution.py:224
  7.4 4.3 %collective-permute-start.4 = (bf16[256,128]{1,0:T(8,128)(2,1)S(1)}, bf16[256,128]{1,0:T(8,128)(2,1)S(1)}, u32[]{:S(2)}, u32[]{:S(2)}) collective-permute-start(bf16[256,128]{1,0:T(8,128)(2,1)S(1)} %constant_dynamic-update-slice_fusion.2.chip), channel_id=1, source_target_pairs={{0,8},{1,9},{2,10},{3,11},{4,5},{5,4},{6,7},{7,6},{8,0},{9,1},{10,... | collective-permute-start | bytes 196616 | tf_op jit(solution)/shard_map/ppermute | solution.py:224
  11.6 4.6 %collective-permute-start.6 = (bf16[512,128]{1,0:T(8,128)(2,1)S(1)}, bf16[512,128]{1,0:T(8,128)(2,1)S(1)}, u32[]{:S(2)}, u32[]{:S(2)}) collective-permute-start(bf16[512,128]{1,0:T(8,128)(2,1)S(1)} %constant_dynamic-update-slice_fusion.near), channel_id=1, source_target_pairs={{0,4},{1,5},{2,6},{3,7},{4,0},{5,1},{6,2},{7,3},{8,12},{9,13},{10,... | collective-permute-start | bytes 393224 | tf_op jit(solution)/shard_map/ppermute | solution.py:224
  11.7 3.6 %collective-permute-start.5 = (bf16[256,128]{1,0:T(8,128)(2,1)S(1)}, bf16[256,128]{1,0:T(8,128)(2,1)S(1)}, u32[]{:S(2)}, u32[]{:S(2)}) collective-permute-start(bf16[256,128]{1,0:T(8,128)(2,1)S(1)} %collective-permute-done.1.near), channel_id=1, source_target_pairs={{0,4},{1,5},{2,6},{3,7},{4,0},{5,1},{6,2},{7,3},{8,12},{9,13},{10,... | collective-permute-start | bytes 196616 | tf_op jit(solution)/shard_map/ppermute | solution.py:224
  12.2 1.2 %copy-start = (bf16[512,8,1,128]{3,1,2,0:T(8,128)(2,1)S(1)}, bf16[512,8,1,128]{3,1,2,0:T(8,128)(2,1)}, u32[]{:S(2)}) copy-start(bf16[512,8,1,128]{3,1,2,0:T(8,128)(2,1)} %param.4) | copy-start | bytes 3145732
  17.1 5.2 %collective-permute-start.7 = (bf16[256,128]{1,0:T(8,128)(2,1)S(1)}, bf16[256,128]{1,0:T(8,128)(2,1)S(1)}, u32[]{:S(2)}, u32[]{:S(2)}) collective-permute-start(bf16[256,128]{1,0:T(8,128)(2,1)S(1)} %get-tuple-element.28), channel_id=1, source_target_pairs={{0,24},{1,25},{2,26},{3,27},{4,7},{5,6},{6,5},{7,4},{8,16},{9,17},... | collective-permute-start | bytes 196616 | tf_op jit(solution)/shard_map/ppermute | solution.py:224
  19.2 4.3 %collective-permute-start.8 = (bf16[256,128]{1,0:T(8,128)(2,1)S(1)}, bf16[256,128]{1,0:T(8,128)(2,1)S(1)}, u32[]{:S(2)}, u32[]{:S(2)}) collective-permute-start(bf16[256,128]{1,0:T(8,128)(2,1)S(1)} %get-tuple-element.29), channel_id=1, source_target_pairs={{0,16},{1,17},{2,18},{3,19},{4,6},{5,7},{6,4},{7,5},{8,24},{9,25},... | collective-permute-start | bytes 196616 | tf_op jit(solution)/shard_map/ppermute | solution.py:224
  19.7 4.3 %collective-permute-start.9 = (bf16[256,128]{1,0:T(8,128)(2,1)S(1)}, bf16[256,128]{1,0:T(8,128)(2,1)S(1)}, u32[]{:S(2)}, u32[]{:S(2)}) collective-permute-start(bf16[256,128]{1,0:T(8,128)(2,1)S(1)} %get-tuple-element.30), channel_id=1, source_target_pairs={{0,8},{1,9},{2,10},{3,11},{4,5},{5,4},{6,7},{7,6},{8,0},{9,1},{10,... | collective-permute-start | bytes 196616 | tf_op jit(solution)/shard_map/ppermute | solution.py:224
  24.0 1.3 %collective-permute-start.10 = (f32[128,128]{1,0:T(8,128)S(1)}, f32[128,128]{1,0:T(8,128)S(1)}, u32[]{:S(2)}, u32[]{:S(2)}) collective-permute-start(f32[128,128]{1,0:T(8,128)S(1)} %get-tuple-element.32), channel_id=1, source_target_pairs={{0,4},{1,5},{2,6},{3,7},{4,0},{5,1},{6,2},{7,3},{8,12},{9,13},{10,... | collective-permute-start | bytes 196616 | tf_op jit(solution)/shard_map/ppermute | solution.py:224

commit v4 on v3

--- a/solution.py
+++ b/solution.py
@@ -17,7 +17,7 @@
 
 
 def origin(i, distance, n):
-    return i ^ distance if n & (n - 1) == 0 else lax.rem(i + n - distance, n)
+    return i ^ distance if n & (n - 1) == 0 else (i + n - distance) % n
 
 
 def dot(a, b, over):
@@ -73,7 +73,7 @@
     def piece(self, tiles, line, plane):
         at = pl.ds(pl.multiple_of(line * self.pts, self.pts), self.pts)
         cols = pl.ds(pl.multiple_of(plane * self.chip, self.chip), self.chip)
-        return jnp.concatenate([tile[at, cols] for tile in tiles], 0)
+        return jnp.concatenate([tile[at, cols] for tile in tiles], 0).astype(F32)
 
     def term(self, core, tiles, mine, at, theirs, theirs_at):
         if not core and len(at) > 1 and len(theirs_at) > 1:
@@ -117,7 +117,8 @@
             for k in self.blocks(core, 0, 2):
                 block = augmented(near[...] if k else chip[...], inv[...], bool(core))
                 mine[self.rows(k), :] = block
-                part[self.rows(k), :] = self.add(core, chip_of, tiles, block, [k], side, [0])
+                total = self.add(core, chip_of, tiles, block, [k], side, [0])
+                part[self.rows(k), :] = self.closed(block, total)
 
         self.on_each_core(body)
 
@@ -133,12 +134,14 @@
                 rows = self.rows(ks[0] - 2, len(ks))
                 block = augmented(near[rows, :], inv[...], bool(core))
                 mine[rows, :] = block
-                part[rows, :] = self.add(core, chip_of, tiles, block, ks, sides, [0] + new)
+                total = self.add(core, chip_of, tiles, block, ks, sides, [0] + new)
+                part[rows, :] = self.closed(block, total)
             ks = self.blocks(core, 0, 2)
             rows = self.rows(0, len(ks))
             total = part0[rows, :]
             if new:
-                total += self.add(core, chip_of, tiles, mine0[rows, :], ks, side, new)
+                block = mine0[rows, :]
+                total += self.closed(block, self.add(core, chip_of, tiles, block, ks, side, new))
             first[rows, :] = total
 
         self.on_each_core(body)
@@ -160,19 +163,19 @@
             for ks in self.groups(core, 1, self.steps + 1):
                 parts = [(mine0, first, k) if k == 1 else (mine, part, k - 2) for k in ks]
                 block = jnp.concatenate([m[self.rows(at), :] for m, _, at in parts], 0)
-                total = jnp.concatenate([p[self.rows(at), :] for _, p, at in parts], 0)
                 if few:
-                    total += self.add(core, chip_of, tiles, block, ks, side, have)
+                    total = self.add(core, chip_of, tiles, block, ks, side, have)
                 else:
-                    total = self.rest(core, chip_of, tiles, block, ks, theirs, have, total)
+                    total = self.rest(core, chip_of, tiles, block, ks, theirs, have)
                 value = self.closed(block, total)
+                value += jnp.concatenate([p[self.rows(at), :] for _, p, at in parts], 0)
                 for n, k in enumerate(ks):
                     out = outs[k - 1]
                     out[...] = value[n * self.chip : (n + 1) * self.chip].astype(out.dtype)
 
         self.on_each_core(body)
 
-    def rest(self, core, chip_of, tiles, block, ks, theirs, have, total):
+    def rest(self, core, chip_of, tiles, block, ks, theirs, have):
         def step(j, total):
             rows = pl.ds(pl.multiple_of((j - 2) * self.chip, self.chip), self.chip)
             side = theirs[rows, :]
@@ -182,19 +185,20 @@
             at = [chip_of(core, k) for k in ks]
             return total + self.term(core, tiles, block, at, side, [from_at])
 
-        return lax.fori_loop(have[0], have[-1] + 1, step, total)
+        zero = jnp.zeros((block.shape[0], 2 * self.width), F32)
+        return lax.fori_loop(have[0], have[-1] + 1, step, zero)
 
     def keep(self, mine0, first, theirs, a_own, a_other, out):
         def body(core, chip_of):
             tiles = (a_other, a_own) if core else (a_own, a_other)
-            block, total = mine0[self.rows(0), :], first[self.rows(0), :]
+            block = mine0[self.rows(0), :]
             have = self.blocks(1 - core, 2, self.steps + 1)
             if len(have) <= 3:
                 side = theirs[self.rows(have[0] - 2, len(have)), :]
-                total += self.add(core, chip_of, tiles, block, [0], side, have)
+                total = self.add(core, chip_of, tiles, block, [0], side, have)
             else:
-                total = self.rest(core, chip_of, tiles, block, [0], theirs, have, total)
-            out[...] = self.closed(block, total)
+                total = self.rest(core, chip_of, tiles, block, [0], theirs, have)
+            out[...] = first[self.rows(0), :] + self.closed(block, total)
 
         self.on_each_core(body)
 
@@ -226,13 +230,13 @@
     def swap(value):
         return permute(value, lambda r, c: (r ^ 1, c))
 
-    def exchange(value, k):
+    def exchange(value, k, to):
         distance = steps + 1 - k
 
         def target(r, c):
             if r % 2:
-                return r, partner(c, (distance - 1) % (lines - 1) + 1, lines)
-            return 2 * partner(r // 2, (distance - 1) % (planes - 1) + 1, planes), c
+                return r, to(c, (distance - 1) % (lines - 1) + 1, lines)
+            return 2 * to(r // 2, (distance - 1) % (planes - 1) + 1, planes), c
 
         return permute(value, target)
 
@@ -261,7 +265,7 @@
         chip = lax.dynamic_update_slice(chip, other, ((1 - core) * pts, 0))
         near = []
         for k in range(1, steps + 1):
-            near.append(exchange(chip, k))
+            near.append(exchange(chip, k, partner))
         count, wide = abar.shape[0], abar.shape[1] * abar.shape[2]
         cells = [a.reshape(count * wide, abar.shape[3]) for a in (abar, abar_other)]
         if count <= 8 * pts:
@@ -276,14 +280,14 @@
                 name="relayout",
             )(*cells)
         else:
-            tiles = [a.reshape(count, wide * width).astype(F32) for a in cells]
+            tiles = [a.reshape(count, wide * width) for a in cells]
         far1 = swap(near[0])
         after = jnp.concatenate(near[1:], 0)
         far2 = swap(after)
         deep = 2 * width
         mine0, theirs0, part0 = call(
             lay.early,
-            [((2 * chip_rows, deep), BF16), ((chip_rows, deep), BF16), ((2 * chip_rows, deep), F32)],
+            [((2 * chip_rows, deep), BF16), ((chip_rows, deep), BF16), ((2 * chip_rows, width), F32)],
             chip,
             inv,
             near[0],
@@ -294,8 +298,8 @@
             lay.middle,
             [
                 ((rest_rows, deep), BF16),
-                ((2 * chip_rows, deep), F32),
-                ((rest_rows, deep), F32),
+                ((2 * chip_rows, width), F32),
+                ((rest_rows, width), F32),
             ],
             inv,
             after,
@@ -318,7 +322,7 @@
         )
         got = []
         for k in range(1, steps + 1):
-            got.append(exchange(outs[k - 1], k))
+            got.append(exchange(outs[k - 1], k, origin))
         (out,) = call(lay.keep, [((chip_rows, width), F32)], mine0, first, theirs, *tiles)
         keep, send = call(lay.total, [((pts, width), F32)] * 2, inv, out, *got)
         return keep + swap(send)

time: 26.1 us -> 26.1 us (level)
  no operation moved by 1% of the time
where the time goes in v4:
time: 26.1 us; the launch traced here: 25.9 us
  waiting for transfers between devices  9.52 us (36%)
  starting transfers between devices  9.46 us (36%)
  Pallas kernels  4.18 us (16%)
  local copies, waits for them, and re-layouts  2.04 us (8%)
  other arithmetic  0.64 us (2%)
    ppermute x11, waiting for transfers between devices, permute(): return lax.ppermute(value, AXES, pairs)  9.52 us
    ppermute x11, starting transfers between devices, permute(): return lax.ppermute(value, AXES, pairs)  9.46 us
    pallas_call x5, Pallas kernels, call(): pl.pallas_call(body, out_shape=[jax.ShapeDtypeStruct(s, t) for s, t in ou...  3.19 us
    unnamed x5, local copies, waits for them, and re-layouts  1.23 us
    pallas_call x1, Pallas kernels, local_part(): pl.pallas_call(lambda *refs: relayout(wide, deep, *refs), out_shape=[jax....  0.99 us
    dynamic_update_slice x1, local copies, waits for them, and re-layouts, local_part(): lax.dynamic_update_slice(jnp.zeros((chip_rows, width), points.dtype), poi...  0.77 us
    add x1, other arithmetic, local_part(): return keep + swap(send)  0.64 us
  transfers between devices with their start and end apart: 11, of which 7 were waited for; matrix products, arithmetic and copies ran while one was open for 3% of the time, Pallas kernels for 13%

profile of v4, /device:TPU:0, one launch (start us, length us, event | category | flops | bytes accessed | tf_op | source)
XLA Modules:
  0.0 25.9 jit_solution(7866455399938944754)
XLA Ops:
  0.0 0.0 copy-start.1
  0.0 0.5 %collective-permute-start.2 = (bf16[512,8,1,128]{3,1,2,0:T(8,128)(2,1)}, bf16[512,8,1,128]{3,1,2,0:T(8,128)(2,1)S(1)}, u32[]{:S(2)}, u32[]{:S(2)}) collective-permute-start(bf16[512,8,1,128]{3,1,2,0:T(8,128)(2,1)} %param.4), channel_id=1, source_target_pairs={{0,4},{1,5},{2,6},{3,7},{4,0},{5,1},{6,2},{7,3},{8,12},{9,13},{10,... | collective-permute-start | bytes 3145736 | tf_op jit(solution)/shard_map/ppermute | solution.py:228
  0.5 0.1 collective-permute-start
  0.6 0.8 %constant_dynamic-update-slice_fusion.3 = bf16[256,128]{1,0:T(8,128)(2,1)S(1)} fusion(bf16[256,128]{1,0:T(8,128)(2,1)S(1)} %broadcast_in_dim.7, bf16[128,128]{1,0:T(8,128)(2,1)} %param.3, s32[]{:T(128)S(6)} %select_n.14), kind=kLoop, calls=%fused_computation.3 | loop fusion | bytes 65540 | tf_op jit(solution)/shard_map/dynamic_update_slice | solution.py:262
  1.3 1.7 %collective-permute-done = bf16[128,128]{1,0:T(8,128)(2,1)S(1)} collective-permute-done((bf16[128,128]{1,0:T(8,128)(2,1)}, bf16[128,128]{1,0:T(8,128)(2,1)S(1)}, u32[]{:S(2)}, u32[]{:S(2)}) %collective-permute-start) | collective-permute-done | bytes 32800 | tf_op jit(solution)/shard_map/ppermute | solution.py:228
  3.0 2.9 %collective-permute-start.3 = (bf16[256,128]{1,0:T(8,128)(2,1)S(1)}, bf16[256,128]{1,0:T(8,128)(2,1)S(1)}, u32[]{:S(2)}, u32[]{:S(2)}) collective-permute-start(bf16[256,128]{1,0:T(8,128)(2,1)S(1)} %constant_dynamic-update-slice_fusion.2.chip), channel_id=1, source_target_pairs={{0,16},{1,17},{2,18},{3,19},{4,6},{5,7},{6,4},{7,5},{8,24},{9,25},... | collective-permute-start | bytes 196616 | tf_op jit(solution)/shard_map/ppermute | solution.py:228
  5.9 1.4 %collective-permute-start.1 = (bf16[256,128]{1,0:T(8,128)(2,1)S(1)}, bf16[256,128]{1,0:T(8,128)(2,1)S(1)}, u32[]{:S(2)}, u32[]{:S(2)}) collective-permute-start(bf16[256,128]{1,0:T(8,128)(2,1)S(1)} %constant_dynamic-update-slice_fusion.2.chip), channel_id=1, source_target_pairs={{0,24},{1,25},{2,26},{3,27},{4,7},{5,6},{6,5},{7,4},{8,16},{9,17},... | collective-permute-start | bytes 196616 | tf_op jit(solution)/shard_map/ppermute | solution.py:228
  7.4 0.1 collective-permute-start.4
  7.5 0.7 %collective-permute-done.3 = bf16[256,128]{1,0:T(8,128)(2,1)S(1)} collective-permute-done((bf16[256,128]{1,0:T(8,128)(2,1)S(1)}, bf16[256,128]{1,0:T(8,128)(2,1)S(1)}, u32[]{:S(2)}, u32[]{:S(2)}) %collective-permute-start.3) | collective-permute-done | bytes 65568 | tf_op jit(solution)/shard_map/ppermute | solution.py:228
  8.2 3.5 %collective-permute-done.4 = bf16[256,128]{1,0:T(8,128)(2,1)S(1)} collective-permute-done((bf16[256,128]{1,0:T(8,128)(2,1)S(1)}, bf16[256,128]{1,0:T(8,128)(2,1)S(1)}, u32[]{:S(2)}, u32[]{:S(2)}) %collective-permute-start.4) | collective-permute-done | bytes 65568 | tf_op jit(solution)/shard_map/ppermute | solution.py:228
  11.6 0.1 collective-permute-start.6
  11.7 0.0 collective-permute-done.1.near
  11.7 0.5 %collective-permute-start.5 = (bf16[256,128]{1,0:T(8,128)(2,1)S(1)}, bf16[256,128]{1,0:T(8,128)(2,1)S(1)}, u32[]{:S(2)}, u32[]{:S(2)}) collective-permute-start(bf16[256,128]{1,0:T(8,128)(2,1)S(1)} %collective-permute-done.1.near), channel_id=1, source_target_pairs={{0,4},{1,5},{2,6},{3,7},{4,0},{5,1},{6,2},{7,3},{8,12},{9,13},{10,... | collective-permute-start | bytes 196616 | tf_op jit(solution)/shard_map/ppermute | solution.py:228
  12.2 0.0 collective-permute-done.2
  12.2 0.0 copy-start
  12.2 1.2 %copy-done = bf16[512,8,1,128]{3,1,2,0:T(8,128)(2,1)S(1)} copy-done((bf16[512,8,1,128]{3,1,2,0:T(8,128)(2,1)S(1)}, bf16[512,8,1,128]{3,1,2,0:T(8,128)(2,1)}, u32[]{:S(2)}) %copy-start) | copy-done | bytes 1048600
  13.4 1.0 %relayout.1 = (f32[512,1024]{1,0:T(8,128)S(1)}, f32[512,1024]{1,0:T(8,128)S(1)}) custom-call(bf16[4096,128]{1,0:T(8,128)(2,1)S(1)} %bitcast.3, bf16[4096,128]{1,0:T(8,128)(2,1)S(1)} %bitcast.4), custom_call_target="tpu_custom_call" | custom-call | tf_op jit(solution)/shard_map/relayout/pallas_call | solution.py:273
  14.4 0.0 copy-done.1
  14.5 0.9 %shard_map.37 = (bf16[512,256]{1,0:T(8,128)(2,1)S(1)}, bf16[256,256]{1,0:T(8,128)(2,1)S(1)}, f32[512,128]{1,0:T(8,128)S(1)}) custom-call(bf16[256,128]{1,0:T(8,128)(2,1)S(1)} %constant_dynamic-update-slice_fusion.2.chip, f32[1,128]{1,0:T(1,128)S(1)} %bitcast.5, bf16[256,128]{1,0:T(8,128)(2,1)S(1)} %collective-permute-done.1.near, ...), custom_call_target="tpu_custom_call" | custom-call | tf_op jit(solution)/shard_map/pallas_call | solution.py:252
  15.4 0.0 collective-permute-done.5.far
  15.4 0.9 %shard_map.38 = (bf16[512,256]{1,0:T(8,128)(2,1)S(1)}, f32[512,128]{1,0:T(8,128)S(1)}, f32[512,128]{1,0:T(8,128)S(1)}) custom-call(f32[1,128]{1,0:T(1,128)S(1)} %bitcast.6, bf16[512,128]{1,0:T(8,128)(2,1)S(1)} %constant_dynamic-update-slice_fusion.near, bf16[256,128]{1,0:T(8,128)(2,1)S(1)} %collective-permute-done.5.far, ...), custom_call_target="tpu_custom_call" | custom-call | tf_op jit(solution)/shard_map/pallas_call | solution.py:252
  16.3 0.0 collective-permute-done.6.far
  16.3 0.8 %shard_map.39 = (bf16[512,256]{1,0:T(8,128)(2,1)S(1)}, bf16[256,128]{1,0:T(8,128)(2,1)S(1)}, bf16[256,128]{1,0:T(8,128)(2,1)S(1)}, bf16[256,128]{1,0:T(8,128)(2,1)S(1)}) custom-call(f32[1,128]{1,0:T(1,128)S(1)} %bitcast.7, bf16[512,128]{1,0:T(8,128)(2,1)S(1)} %collective-permute-done.6.far, bf16[512,256]{1,0:T(8,128)(2,1)S(1)} %get-tuple-element.21.mine0, ...), custom_call_target="tpu_custom_call" | custom-call | tf_op jit(solution)/shard_map/pallas_call | solution.py:252
  17.1 2.1 %collective-permute-start.7 = (bf16[256,128]{1,0:T(8,128)(2,1)S(1)}, bf16[256,128]{1,0:T(8,128)(2,1)S(1)}, u32[]{:S(2)}, u32[]{:S(2)}) collective-permute-start(bf16[256,128]{1,0:T(8,128)(2,1)S(1)} %get-tuple-element.28), channel_id=1, source_target_pairs={{0,24},{1,25},{2,26},{3,27},{4,7},{5,6},{6,5},{7,4},{8,16},{9,17},... | collective-permute-start | bytes 196616 | tf_op jit(solution)/shard_map/ppermute | solution.py:228
  19.2 0.5 %collective-permute-start.8 = (bf16[256,128]{1,0:T(8,128)(2,1)S(1)}, bf16[256,128]{1,0:T(8,128)(2,1)S(1)}, u32[]{:S(2)}, u32[]{:S(2)}) collective-permute-start(bf16[256,128]{1,0:T(8,128)(2,1)S(1)} %get-tuple-element.29), channel_id=1, source_target_pairs={{0,16},{1,17},{2,18},{3,19},{4,6},{5,7},{6,4},{7,5},{8,24},{9,25},... | collective-permute-start | bytes 196616 | tf_op jit(solution)/shard_map/ppermute | solution.py:228
  19.7 1.0 %collective-permute-start.9 = (bf16[256,128]{1,0:T(8,128)(2,1)S(1)}, bf16[256,128]{1,0:T(8,128)(2,1)S(1)}, u32[]{:S(2)}, u32[]{:S(2)}) collective-permute-start(bf16[256,128]{1,0:T(8,128)(2,1)S(1)} %get-tuple-element.30), channel_id=1, source_target_pairs={{0,8},{1,9},{2,10},{3,11},{4,5},{5,4},{6,7},{7,6},{8,0},{9,1},{10,... | collective-permute-start | bytes 196616 | tf_op jit(solution)/shard_map/ppermute | solution.py:228
  20.7 0.5 %shard_map.40.refs_1_ = f32[256,128]{1,0:T(8,128)S(1)} custom-call(bf16[512,256]{1,0:T(8,128)(2,1)S(1)} %get-tuple-element.21.mine0, f32[512,128]{1,0:T(8,128)S(1)} %get-tuple-element.24.first, bf16[512,256]{1,0:T(8,128)(2,1)S(1)} %get-tuple-element.27.theirs, f32[512,1024]{1,0:T(8,128)S(1)} %get-tuple-element.19.a_own, ...), custom_call_target="tpu_custom_call" | custom-call | tf_op jit(solution)/shard_map/pallas_call | solution.py:252
  21.2 1.1 %collective-permute-done.7.refs_2_ = bf16[256,128]{1,0:T(8,128)(2,1)S(1)} collective-permute-done((bf16[256,128]{1,0:T(8,128)(2,1)S(1)}, bf16[256,128]{1,0:T(8,128)(2,1)S(1)}, u32[]{:S(2)}, u32[]{:S(2)}) %collective-permute-start.7) | collective-permute-done | bytes 65568 | tf_op jit(solution)/shard_map/ppermute | solution.py:228
  22.3 1.1 %collective-permute-done.8.refs_3_ = bf16[256,128]{1,0:T(8,128)(2,1)S(1)} collective-permute-done((bf16[256,128]{1,0:T(8,128)(2,1)S(1)}, bf16[256,128]{1,0:T(8,128)(2,1)S(1)}, u32[]{:S(2)}, u32[]{:S(2)}) %collective-permute-start.8) | collective-permute-done | bytes 65568 | tf_op jit(solution)/shard_map/ppermute | solution.py:228
  23.4 0.5 %collective-permute-done.9.refs_4_ = bf16[256,128]{1,0:T(8,128)(2,1)S(1)} collective-permute-done((bf16[256,128]{1,0:T(8,128)(2,1)S(1)}, bf16[256,128]{1,0:T(8,128)(2,1)S(1)}, u32[]{:S(2)}, u32[]{:S(2)}) %collective-permute-start.9) | collective-permute-done | bytes 65568 | tf_op jit(solution)/shard_map/ppermute | solution.py:228
  24.0 0.4 %collective-permute-start.10 = (f32[128,128]{1,0:T(8,128)S(1)}, f32[128,128]{1,0:T(8,128)S(1)}, u32[]{:S(2)}, u32[]{:S(2)}) collective-permute-start(f32[128,128]{1,0:T(8,128)S(1)} %get-tuple-element.32), channel_id=1, source_target_pairs={{0,4},{1,5},{2,6},{3,7},{4,0},{5,1},{6,2},{7,3},{8,12},{9,13},{10,... | collective-permute-start | bytes 196616 | tf_op jit(solution)/shard_map/ppermute | solution.py:228
  24.4 0.9 %collective-permute-done.10 = f32[128,128]{1,0:T(8,128)S(1)} collective-permute-done((f32[128,128]{1,0:T(8,128)S(1)}, f32[128,128]{1,0:T(8,128)S(1)}, u32[]{:S(2)}, u32[]{:S(2)}) %collective-permute-start.10) | collective-permute-done | bytes 65568 | tf_op jit(solution)/shard_map/ppermute | solution.py:228
  25.3 0.6 %add.16 = f32[128,128]{1,0:T(8,128)} add(f32[128,128]{1,0:T(8,128)S(1)} %get-tuple-element.31, f32[128,128]{1,0:T(8,128)S(1)} %collective-permute-done.10) | non-fusion elementwise | flops 16384 | bytes 196608 | tf_op jit(solution)/shard_map/add | solution.py:328
  (5 shorter events, 0.1 us)
Async XLA Ops:
  0.0 14.4 %copy-start.1 = (f32[128]{0:T(128)S(1)}, f32[128]{0:T(128)}, u32[]{:S(2)}) copy-start(f32[128]{0:T(128)} %param.5) | copy-start | bytes 1540
  0.0 12.2 %collective-permute-start.2 = (bf16[512,8,1,128]{3,1,2,0:T(8,128)(2,1)}, bf16[512,8,1,128]{3,1,2,0:T(8,128)(2,1)S(1)}, u32[]{:S(2)}, u32[]{:S(2)}) collective-permute-start(bf16[512,8,1,128]{3,1,2,0:T(8,128)(2,1)} %param.4), channel_id=1, source_target_pairs={{0,4},{1,5},{2,6},{3,7},{4,0},{5,1},{6,2},{7,3},{8,12},{9,13},{10,... | collective-permute-start | bytes 3145736 | tf_op jit(solution)/shard_map/ppermute | solution.py:228
  0.5 2.5 %collective-permute-start = (bf16[128,128]{1,0:T(8,128)(2,1)}, bf16[128,128]{1,0:T(8,128)(2,1)S(1)}, u32[]{:S(2)}, u32[]{:S(2)}) collective-permute-start(bf16[128,128]{1,0:T(8,128)(2,1)} %param.3), channel_id=1, source_target_pairs={{0,4},{1,5},{2,6},{3,7},{4,0},{5,1},{6,2},{7,3},{8,12},{9,13},{10,... | collective-permute-start | bytes 98312 | tf_op jit(solution)/shard_map/ppermute | solution.py:228
  3.0 5.1 %collective-permute-start.3 = (bf16[256,128]{1,0:T(8,128)(2,1)S(1)}, bf16[256,128]{1,0:T(8,128)(2,1)S(1)}, u32[]{:S(2)}, u32[]{:S(2)}) collective-permute-start(bf16[256,128]{1,0:T(8,128)(2,1)S(1)} %constant_dynamic-update-slice_fusion.2.chip), channel_id=1, source_target_pairs={{0,16},{1,17},{2,18},{3,19},{4,6},{5,7},{6,4},{7,5},{8,24},{9,25},... | collective-permute-start | bytes 196616 | tf_op jit(solution)/shard_map/ppermute | solution.py:228
  5.9 5.8 %collective-permute-start.1 = (bf16[256,128]{1,0:T(8,128)(2,1)S(1)}, bf16[256,128]{1,0:T(8,128)(2,1)S(1)}, u32[]{:S(2)}, u32[]{:S(2)}) collective-permute-start(bf16[256,128]{1,0:T(8,128)(2,1)S(1)} %constant_dynamic-update-slice_fusion.2.chip), channel_id=1, source_target_pairs={{0,24},{1,25},{2,26},{3,27},{4,7},{5,6},{6,5},{7,4},{8,16},{9,17},... | collective-permute-start | bytes 196616 | tf_op jit(solution)/shard_map/ppermute | solution.py:228
  7.4 4.3 %collective-permute-start.4 = (bf16[256,128]{1,0:T(8,128)(2,1)S(1)}, bf16[256,128]{1,0:T(8,128)(2,1)S(1)}, u32[]{:S(2)}, u32[]{:S(2)}) collective-permute-start(bf16[256,128]{1,0:T(8,128)(2,1)S(1)} %constant_dynamic-update-slice_fusion.2.chip), channel_id=1, source_target_pairs={{0,8},{1,9},{2,10},{3,11},{4,5},{5,4},{6,7},{7,6},{8,0},{9,1},{10,... | collective-permute-start | bytes 196616 | tf_op jit(solution)/shard_map/ppermute | solution.py:228
  11.6 4.6 %collective-permute-start.6 = (bf16[512,128]{1,0:T(8,128)(2,1)S(1)}, bf16[512,128]{1,0:T(8,128)(2,1)S(1)}, u32[]{:S(2)}, u32[]{:S(2)}) collective-permute-start(bf16[512,128]{1,0:T(8,128)(2,1)S(1)} %constant_dynamic-update-slice_fusion.near), channel_id=1, source_target_pairs={{0,4},{1,5},{2,6},{3,7},{4,0},{5,1},{6,2},{7,3},{8,12},{9,13},{10,... | collective-permute-start | bytes 393224 | tf_op jit(solution)/shard_map/ppermute | solution.py:228
  11.7 3.6 %collective-permute-start.5 = (bf16[256,128]{1,0:T(8,128)(2,1)S(1)}, bf16[256,128]{1,0:T(8,128)(2,1)S(1)}, u32[]{:S(2)}, u32[]{:S(2)}) collective-permute-start(bf16[256,128]{1,0:T(8,128)(2,1)S(1)} %collective-permute-done.1.near), channel_id=1, source_target_pairs={{0,4},{1,5},{2,6},{3,7},{4,0},{5,1},{6,2},{7,3},{8,12},{9,13},{10,... | collective-permute-start | bytes 196616 | tf_op jit(solution)/shard_map/ppermute | solution.py:228
  12.2 1.2 %copy-start = (bf16[512,8,1,128]{3,1,2,0:T(8,128)(2,1)S(1)}, bf16[512,8,1,128]{3,1,2,0:T(8,128)(2,1)}, u32[]{:S(2)}) copy-start(bf16[512,8,1,128]{3,1,2,0:T(8,128)(2,1)} %param.4) | copy-start | bytes 3145732
  17.1 5.2 %collective-permute-start.7 = (bf16[256,128]{1,0:T(8,128)(2,1)S(1)}, bf16[256,128]{1,0:T(8,128)(2,1)S(1)}, u32[]{:S(2)}, u32[]{:S(2)}) collective-permute-start(bf16[256,128]{1,0:T(8,128)(2,1)S(1)} %get-tuple-element.28), channel_id=1, source_target_pairs={{0,24},{1,25},{2,26},{3,27},{4,7},{5,6},{6,5},{7,4},{8,16},{9,17},... | collective-permute-start | bytes 196616 | tf_op jit(solution)/shard_map/ppermute | solution.py:228
  19.2 4.3 %collective-permute-start.8 = (bf16[256,128]{1,0:T(8,128)(2,1)S(1)}, bf16[256,128]{1,0:T(8,128)(2,1)S(1)}, u32[]{:S(2)}, u32[]{:S(2)}) collective-permute-start(bf16[256,128]{1,0:T(8,128)(2,1)S(1)} %get-tuple-element.29), channel_id=1, source_target_pairs={{0,16},{1,17},{2,18},{3,19},{4,6},{5,7},{6,4},{7,5},{8,24},{9,25},... | collective-permute-start | bytes 196616 | tf_op jit(solution)/shard_map/ppermute | solution.py:228
  19.7 4.3 %collective-permute-start.9 = (bf16[256,128]{1,0:T(8,128)(2,1)S(1)}, bf16[256,128]{1,0:T(8,128)(2,1)S(1)}, u32[]{:S(2)}, u32[]{:S(2)}) collective-permute-start(bf16[256,128]{1,0:T(8,128)(2,1)S(1)} %get-tuple-element.30), channel_id=1, source_target_pairs={{0,8},{1,9},{2,10},{3,11},{4,5},{5,4},{6,7},{7,6},{8,0},{9,1},{10,... | collective-permute-start | bytes 196616 | tf_op jit(solution)/shard_map/ppermute | solution.py:228
  24.0 1.3 %collective-permute-start.10 = (f32[128,128]{1,0:T(8,128)S(1)}, f32[128,128]{1,0:T(8,128)S(1)}, u32[]{:S(2)}, u32[]{:S(2)}) collective-permute-start(f32[128,128]{1,0:T(8,128)S(1)} %get-tuple-element.32), channel_id=1, source_target_pairs={{0,4},{1,5},{2,6},{3,7},{4,0},{5,1},{6,2},{7,3},{8,12},{9,13},{10,... | collective-permute-start | bytes 196616 | tf_op jit(solution)/shard_map/ppermute | solution.py:228

commit v5 on v3

--- a/solution.py
+++ b/solution.py
@@ -146,14 +146,16 @@
     def closed(self, block, total):
         return total[:, self.width :] * block[:, : self.width].astype(F32) - total[:, : self.width]
 
-    def send(self, inv, far, mine0, mine, first, part, a_own, a_other, theirs, *outs):
+    def send(self, inv, far, mine0, mine, first, part, a_own, a_other, *outs):
         def body(core, chip_of):
             tiles = (a_other, a_own) if core else (a_own, a_other)
             have = self.blocks(1 - core, 2, self.steps + 1)
-            few = len(have) <= 3
+            few = self.steps <= 4
+            theirs = None if few else outs[-1]
             given = self.rows(have[0] - 2, len(have))
             side = augmented(far[given, :], inv[...], not core)
-            theirs[given, :] = side
+            if not few:
+                theirs[given, :] = side
             for k in range(1, self.steps + 1):
                 if k not in self.blocks(core, 1, self.steps + 1):
                     outs[k - 1][...] = jnp.zeros(outs[k - 1].shape, outs[k - 1].dtype)
@@ -184,13 +186,14 @@
 
         return lax.fori_loop(have[0], have[-1] + 1, step, total)
 
-    def keep(self, mine0, first, theirs, a_own, a_other, out):
+    def keep(self, inv, mine0, first, theirs, a_own, a_other, out):
         def body(core, chip_of):
             tiles = (a_other, a_own) if core else (a_own, a_other)
             block, total = mine0[self.rows(0), :], first[self.rows(0), :]
             have = self.blocks(1 - core, 2, self.steps + 1)
-            if len(have) <= 3:
-                side = theirs[self.rows(have[0] - 2, len(have)), :]
+            if self.steps <= 4:
+                raw = theirs[self.rows(have[0] - 2, len(have)), :]
+                side = augmented(raw, inv[...], not core)
                 total += self.add(core, chip_of, tiles, block, [0], side, have)
             else:
                 total = self.rest(core, chip_of, tiles, block, [0], theirs, have, total)
@@ -207,7 +210,7 @@
             acc = terms[0][rows, :].astype(F32)
             for term in terms[1:]:
                 acc += term[rows, :].astype(F32)
-            ref[...] = -acc * inv[...]
+            ref[...] = (-acc * inv[...]).astype(ref.dtype)
 
 
 def solution(mesh):
@@ -305,9 +308,9 @@
             part0,
             *tiles,
         )
-        theirs, *outs = call(
+        outs = call(
             lay.send,
-            [((rest_rows, deep), BF16)] + [((chip_rows, width), BF16)] * steps,
+            [((chip_rows, width), BF16)] * steps + [((rest_rows, deep), BF16)] * (steps > 4),
             inv,
             far2,
             mine0,
@@ -319,9 +322,9 @@
         got = []
         for k in range(1, steps + 1):
             got.append(exchange(outs[k - 1], k))
-        (out,) = call(lay.keep, [((chip_rows, width), F32)], mine0, first, theirs, *tiles)
-        keep, send = call(lay.total, [((pts, width), F32)] * 2, inv, out, *got)
-        return keep + swap(send)
+        (out,) = call(lay.keep, [((chip_rows, width), F32)], inv, mine0, first, far2 if steps <= 4 else outs[-1], *tiles)
+        keep, send = call(lay.total, [((pts, width), F32), ((pts, width), BF16)], inv, out, *got)
+        return keep + swap(send).astype(F32)
 
     placed = (P(("row", "col"), None), P("row", None, "col", None), P())
     return jax.shard_map(

time: 26.1 us -> 26.1 us (level)
  no operation moved by 1% of the time
where the time goes in v5:
time: 26.1 us; the launch traced here: 25.9 us
  waiting for transfers between devices  9.47 us (36%)
  starting transfers between devices  9.44 us (36%)
  Pallas kernels  4.2 us (16%)
  local copies, waits for them, and re-layouts  2.04 us (8%)
  other arithmetic  0.64 us (2%)
    ppermute x11, waiting for transfers between devices, permute(): return lax.ppermute(value, AXES, pairs)  9.47 us
    ppermute x11, starting transfers between devices, permute(): return lax.ppermute(value, AXES, pairs)  9.44 us
    pallas_call x5, Pallas kernels, call(): pl.pallas_call(body, out_shape=[jax.ShapeDtypeStruct(s, t) for s, t in ou...  3.21 us
    unnamed x5, local copies, waits for them, and re-layouts  1.23 us
    pallas_call x1, Pallas kernels, local_part(): pl.pallas_call(lambda *refs: relayout(wide, deep, *refs), out_shape=[jax....  0.99 us
    dynamic_update_slice x1, local copies, waits for them, and re-layouts, local_part(): lax.dynamic_update_slice(jnp.zeros((chip_rows, width), points.dtype), poi...  0.77 us
    add x1, other arithmetic, local_part(): return keep + swap(send).astype(F32)  0.64 us
  transfers between devices with their start and end apart: 11, of which 7 were waited for; matrix products, arithmetic and copies ran while one was open for 3% of the time, Pallas kernels for 13%

profile of v5, /device:TPU:0, one launch (start us, length us, event | category | flops | bytes accessed | tf_op | source)
XLA Modules:
  0.0 25.9 jit_solution(6454653770341833490)
XLA Ops:
  0.0 0.0 copy-start.1
  0.0 0.5 %collective-permute-start.2 = (bf16[512,8,1,128]{3,1,2,0:T(8,128)(2,1)}, bf16[512,8,1,128]{3,1,2,0:T(8,128)(2,1)S(1)}, u32[]{:S(2)}, u32[]{:S(2)}) collective-permute-start(bf16[512,8,1,128]{3,1,2,0:T(8,128)(2,1)} %param.4), channel_id=1, source_target_pairs={{0,4},{1,5},{2,6},{3,7},{4,0},{5,1},{6,2},{7,3},{8,12},{9,13},{10,... | collective-permute-start | bytes 3145736 | tf_op jit(solution)/shard_map/ppermute | solution.py:227
  0.5 0.1 collective-permute-start
  0.6 0.8 %constant_dynamic-update-slice_fusion.3 = bf16[256,128]{1,0:T(8,128)(2,1)S(1)} fusion(bf16[256,128]{1,0:T(8,128)(2,1)S(1)} %broadcast_in_dim.7, bf16[128,128]{1,0:T(8,128)(2,1)} %param.3, s32[]{:T(128)S(6)} %select_n.14), kind=kLoop, calls=%fused_computation.4 | loop fusion | bytes 65540 | tf_op jit(solution)/shard_map/dynamic_update_slice | solution.py:261
  1.3 1.7 %collective-permute-done = bf16[128,128]{1,0:T(8,128)(2,1)S(1)} collective-permute-done((bf16[128,128]{1,0:T(8,128)(2,1)}, bf16[128,128]{1,0:T(8,128)(2,1)S(1)}, u32[]{:S(2)}, u32[]{:S(2)}) %collective-permute-start) | collective-permute-done | bytes 32800 | tf_op jit(solution)/shard_map/ppermute | solution.py:227
  3.0 2.9 %collective-permute-start.3 = (bf16[256,128]{1,0:T(8,128)(2,1)S(1)}, bf16[256,128]{1,0:T(8,128)(2,1)S(1)}, u32[]{:S(2)}, u32[]{:S(2)}) collective-permute-start(bf16[256,128]{1,0:T(8,128)(2,1)S(1)} %constant_dynamic-update-slice_fusion.2.chip), channel_id=1, source_target_pairs={{0,16},{1,17},{2,18},{3,19},{4,6},{5,7},{6,4},{7,5},{8,24},{9,25},... | collective-permute-start | bytes 196616 | tf_op jit(solution)/shard_map/ppermute | solution.py:227
  5.9 1.4 %collective-permute-start.1 = (bf16[256,128]{1,0:T(8,128)(2,1)S(1)}, bf16[256,128]{1,0:T(8,128)(2,1)S(1)}, u32[]{:S(2)}, u32[]{:S(2)}) collective-permute-start(bf16[256,128]{1,0:T(8,128)(2,1)S(1)} %constant_dynamic-update-slice_fusion.2.chip), channel_id=1, source_target_pairs={{0,24},{1,25},{2,26},{3,27},{4,7},{5,6},{6,5},{7,4},{8,16},{9,17},... | collective-permute-start | bytes 196616 | tf_op jit(solution)/shard_map/ppermute | solution.py:227
  7.4 0.1 collective-permute-start.4
  7.5 0.7 %collective-permute-done.3 = bf16[256,128]{1,0:T(8,128)(2,1)S(1)} collective-permute-done((bf16[256,128]{1,0:T(8,128)(2,1)S(1)}, bf16[256,128]{1,0:T(8,128)(2,1)S(1)}, u32[]{:S(2)}, u32[]{:S(2)}) %collective-permute-start.3) | collective-permute-done | bytes 65568 | tf_op jit(solution)/shard_map/ppermute | solution.py:227
  8.2 3.5 %collective-permute-done.4 = bf16[256,128]{1,0:T(8,128)(2,1)S(1)} collective-permute-done((bf16[256,128]{1,0:T(8,128)(2,1)S(1)}, bf16[256,128]{1,0:T(8,128)(2,1)S(1)}, u32[]{:S(2)}, u32[]{:S(2)}) %collective-permute-start.4) | collective-permute-done | bytes 65568 | tf_op jit(solution)/shard_map/ppermute | solution.py:227
  11.6 0.1 collective-permute-start.6
  11.7 0.0 collective-permute-done.1.near
  11.7 0.5 %collective-permute-start.5 = (bf16[256,128]{1,0:T(8,128)(2,1)S(1)}, bf16[256,128]{1,0:T(8,128)(2,1)S(1)}, u32[]{:S(2)}, u32[]{:S(2)}) collective-permute-start(bf16[256,128]{1,0:T(8,128)(2,1)S(1)} %collective-permute-done.1.near), channel_id=1, source_target_pairs={{0,4},{1,5},{2,6},{3,7},{4,0},{5,1},{6,2},{7,3},{8,12},{9,13},{10,... | collective-permute-start | bytes 196616 | tf_op jit(solution)/shard_map/ppermute | solution.py:227
  12.2 0.0 collective-permute-done.2
  12.2 0.0 copy-start
  12.2 1.2 %copy-done = bf16[512,8,1,128]{3,1,2,0:T(8,128)(2,1)S(1)} copy-done((bf16[512,8,1,128]{3,1,2,0:T(8,128)(2,1)S(1)}, bf16[512,8,1,128]{3,1,2,0:T(8,128)(2,1)}, u32[]{:S(2)}) %copy-start) | copy-done | bytes 1048600
  13.4 1.0 %relayout.1 = (f32[512,1024]{1,0:T(8,128)S(1)}, f32[512,1024]{1,0:T(8,128)S(1)}) custom-call(bf16[4096,128]{1,0:T(8,128)(2,1)S(1)} %bitcast.3, bf16[4096,128]{1,0:T(8,128)(2,1)S(1)} %bitcast.4), custom_call_target="tpu_custom_call" | custom-call | tf_op jit(solution)/shard_map/relayout/pallas_call | solution.py:272
  14.4 0.0 copy-done.1
  14.5 0.9 %shard_map.37 = (bf16[512,256]{1,0:T(8,128)(2,1)S(1)}, bf16[256,256]{1,0:T(8,128)(2,1)S(1)}, f32[512,256]{1,0:T(8,128)S(1)}) custom-call(bf16[256,128]{1,0:T(8,128)(2,1)S(1)} %constant_dynamic-update-slice_fusion.2.chip, f32[1,128]{1,0:T(1,128)S(1)} %bitcast.5, bf16[256,128]{1,0:T(8,128)(2,1)S(1)} %collective-permute-done.1.near, ...), custom_call_target="tpu_custom_call" | custom-call | tf_op jit(solution)/shard_map/pallas_call | solution.py:251
  15.4 0.0 collective-permute-done.5.far
  15.4 0.9 %shard_map.38 = (bf16[512,256]{1,0:T(8,128)(2,1)S(1)}, f32[512,256]{1,0:T(8,128)S(1)}, f32[512,256]{1,0:T(8,128)S(1)}) custom-call(f32[1,128]{1,0:T(1,128)S(1)} %bitcast.6, bf16[512,128]{1,0:T(8,128)(2,1)S(1)} %constant_dynamic-update-slice_fusion.near, bf16[256,128]{1,0:T(8,128)(2,1)S(1)} %collective-permute-done.5.far, ...), custom_call_target="tpu_custom_call" | custom-call | tf_op jit(solution)/shard_map/pallas_call | solution.py:251
  16.3 0.0 collective-permute-done.6.theirs.far
  16.3 0.8 %shard_map.40 = (bf16[256,128]{1,0:T(8,128)(2,1)S(1)}, bf16[256,128]{1,0:T(8,128)(2,1)S(1)}, bf16[256,128]{1,0:T(8,128)(2,1)S(1)}) custom-call(f32[1,128]{1,0:T(1,128)S(1)} %bitcast.7, bf16[512,128]{1,0:T(8,128)(2,1)S(1)} %collective-permute-done.6.theirs.far, bf16[512,256]{1,0:T(8,128)(2,1)S(1)} %get-tuple-element.20.mine0, ...), custom_call_target="tpu_custom_call" | custom-call | tf_op jit(solution)/shard_map/pallas_call | solution.py:251
  17.1 2.1 %collective-permute-start.7 = (bf16[256,128]{1,0:T(8,128)(2,1)S(1)}, bf16[256,128]{1,0:T(8,128)(2,1)S(1)}, u32[]{:S(2)}, u32[]{:S(2)}) collective-permute-start(bf16[256,128]{1,0:T(8,128)(2,1)S(1)} %get-tuple-element.26), channel_id=1, source_target_pairs={{0,24},{1,25},{2,26},{3,27},{4,7},{5,6},{6,5},{7,4},{8,16},{9,17},... | collective-permute-start | bytes 196616 | tf_op jit(solution)/shard_map/ppermute | solution.py:227
  19.2 0.5 %collective-permute-start.8 = (bf16[256,128]{1,0:T(8,128)(2,1)S(1)}, bf16[256,128]{1,0:T(8,128)(2,1)S(1)}, u32[]{:S(2)}, u32[]{:S(2)}) collective-permute-start(bf16[256,128]{1,0:T(8,128)(2,1)S(1)} %get-tuple-element.27), channel_id=1, source_target_pairs={{0,16},{1,17},{2,18},{3,19},{4,6},{5,7},{6,4},{7,5},{8,24},{9,25},... | collective-permute-start | bytes 196616 | tf_op jit(solution)/shard_map/ppermute | solution.py:227
  19.7 1.0 %collective-permute-start.9 = (bf16[256,128]{1,0:T(8,128)(2,1)S(1)}, bf16[256,128]{1,0:T(8,128)(2,1)S(1)}, u32[]{:S(2)}, u32[]{:S(2)}) collective-permute-start(bf16[256,128]{1,0:T(8,128)(2,1)S(1)} %get-tuple-element.28), channel_id=1, source_target_pairs={{0,8},{1,9},{2,10},{3,11},{4,5},{5,4},{6,7},{7,6},{8,0},{9,1},{10,... | collective-permute-start | bytes 196616 | tf_op jit(solution)/shard_map/ppermute | solution.py:227
  20.6 0.6 %shard_map.39.refs_1_ = f32[256,128]{1,0:T(8,128)S(1)} custom-call(f32[1,128]{1,0:T(1,128)S(1)} %bitcast.8, bf16[512,256]{1,0:T(8,128)(2,1)S(1)} %get-tuple-element.20.mine0, f32[512,256]{1,0:T(8,128)S(1)} %get-tuple-element.23.first, bf16[512,128]{1,0:T(8,128)(2,1)S(1)} %collective-permute-done.6.theirs.far, f32[512,1024]{1,0:T(8,128)S(1)} %get-tuple-element.18.a_own, ...), custom_call_target="tpu_custom_call" | custom-call | tf_op jit(solution)/shard_map/pallas_call | solution.py:251
  21.2 1.1 %collective-permute-done.7.refs_2_ = bf16[256,128]{1,0:T(8,128)(2,1)S(1)} collective-permute-done((bf16[256,128]{1,0:T(8,128)(2,1)S(1)}, bf16[256,128]{1,0:T(8,128)(2,1)S(1)}, u32[]{:S(2)}, u32[]{:S(2)}) %collective-permute-start.7) | collective-permute-done | bytes 65568 | tf_op jit(solution)/shard_map/ppermute | solution.py:227
  22.3 1.1 %collective-permute-done.8.refs_3_ = bf16[256,128]{1,0:T(8,128)(2,1)S(1)} collective-permute-done((bf16[256,128]{1,0:T(8,128)(2,1)S(1)}, bf16[256,128]{1,0:T(8,128)(2,1)S(1)}, u32[]{:S(2)}, u32[]{:S(2)}) %collective-permute-start.8) | collective-permute-done | bytes 65568 | tf_op jit(solution)/shard_map/ppermute | solution.py:227
  23.4 0.5 %collective-permute-done.9.refs_4_ = bf16[256,128]{1,0:T(8,128)(2,1)S(1)} collective-permute-done((bf16[256,128]{1,0:T(8,128)(2,1)S(1)}, bf16[256,128]{1,0:T(8,128)(2,1)S(1)}, u32[]{:S(2)}, u32[]{:S(2)}) %collective-permute-start.9) | collective-permute-done | bytes 65568 | tf_op jit(solution)/shard_map/ppermute | solution.py:227
  24.0 0.4 %collective-permute-start.10 = (bf16[128,128]{1,0:T(8,128)(2,1)S(1)}, bf16[128,128]{1,0:T(8,128)(2,1)S(1)}, u32[]{:S(2)}, u32[]{:S(2)}) collective-permute-start(bf16[128,128]{1,0:T(8,128)(2,1)S(1)} %get-tuple-element.30), channel_id=1, source_target_pairs={{0,4},{1,5},{2,6},{3,7},{4,0},{5,1},{6,2},{7,3},{8,12},{9,13},{10,... | collective-permute-start | bytes 98312 | tf_op jit(solution)/shard_map/ppermute | solution.py:227
  24.3 0.9 %collective-permute-done.10 = bf16[128,128]{1,0:T(8,128)(2,1)S(1)} collective-permute-done((bf16[128,128]{1,0:T(8,128)(2,1)S(1)}, bf16[128,128]{1,0:T(8,128)(2,1)S(1)}, u32[]{:S(2)}, u32[]{:S(2)}) %collective-permute-start.10) | collective-permute-done | bytes 32800 | tf_op jit(solution)/shard_map/ppermute | solution.py:227
  25.2 0.6 %convert_add_fusion = f32[128,128]{1,0:T(8,128)} fusion(f32[128,128]{1,0:T(8,128)S(1)} %get-tuple-element.29, bf16[128,128]{1,0:T(8,128)(2,1)S(1)} %collective-permute-done.10), kind=kLoop, calls=%fused_computation | loop fusion | flops 32768 | bytes 163840 | tf_op jit(solution)/shard_map/add | solution.py:327
  (5 shorter events, 0.1 us)
Async XLA Ops:
  0.0 14.4 %copy-start.1 = (f32[128]{0:T(128)S(1)}, f32[128]{0:T(128)}, u32[]{:S(2)}) copy-start(f32[128]{0:T(128)} %param.5) | copy-start | bytes 1540
  0.0 12.2 %collective-permute-start.2 = (bf16[512,8,1,128]{3,1,2,0:T(8,128)(2,1)}, bf16[512,8,1,128]{3,1,2,0:T(8,128)(2,1)S(1)}, u32[]{:S(2)}, u32[]{:S(2)}) collective-permute-start(bf16[512,8,1,128]{3,1,2,0:T(8,128)(2,1)} %param.4), channel_id=1, source_target_pairs={{0,4},{1,5},{2,6},{3,7},{4,0},{5,1},{6,2},{7,3},{8,12},{9,13},{10,... | collective-permute-start | bytes 3145736 | tf_op jit(solution)/shard_map/ppermute | solution.py:227
  0.5 2.5 %collective-permute-start = (bf16[128,128]{1,0:T(8,128)(2,1)}, bf16[128,128]{1,0:T(8,128)(2,1)S(1)}, u32[]{:S(2)}, u32[]{:S(2)}) collective-permute-start(bf16[128,128]{1,0:T(8,128)(2,1)} %param.3), channel_id=1, source_target_pairs={{0,4},{1,5},{2,6},{3,7},{4,0},{5,1},{6,2},{7,3},{8,12},{9,13},{10,... | collective-permute-start | bytes 98312 | tf_op jit(solution)/shard_map/ppermute | solution.py:227
  3.0 5.1 %collective-permute-start.3 = (bf16[256,128]{1,0:T(8,128)(2,1)S(1)}, bf16[256,128]{1,0:T(8,128)(2,1)S(1)}, u32[]{:S(2)}, u32[]{:S(2)}) collective-permute-start(bf16[256,128]{1,0:T(8,128)(2,1)S(1)} %constant_dynamic-update-slice_fusion.2.chip), channel_id=1, source_target_pairs={{0,16},{1,17},{2,18},{3,19},{4,6},{5,7},{6,4},{7,5},{8,24},{9,25},... | collective-permute-start | bytes 196616 | tf_op jit(solution)/shard_map/ppermute | solution.py:227
  5.9 5.8 %collective-permute-start.1 = (bf16[256,128]{1,0:T(8,128)(2,1)S(1)}, bf16[256,128]{1,0:T(8,128)(2,1)S(1)}, u32[]{:S(2)}, u32[]{:S(2)}) collective-permute-start(bf16[256,128]{1,0:T(8,128)(2,1)S(1)} %constant_dynamic-update-slice_fusion.2.chip), channel_id=1, source_target_pairs={{0,24},{1,25},{2,26},{3,27},{4,7},{5,6},{6,5},{7,4},{8,16},{9,17},... | collective-permute-start | bytes 196616 | tf_op jit(solution)/shard_map/ppermute | solution.py:227
  7.4 4.3 %collective-permute-start.4 = (bf16[256,128]{1,0:T(8,128)(2,1)S(1)}, bf16[256,128]{1,0:T(8,128)(2,1)S(1)}, u32[]{:S(2)}, u32[]{:S(2)}) collective-permute-start(bf16[256,128]{1,0:T(8,128)(2,1)S(1)} %constant_dynamic-update-slice_fusion.2.chip), channel_id=1, source_target_pairs={{0,8},{1,9},{2,10},{3,11},{4,5},{5,4},{6,7},{7,6},{8,0},{9,1},{10,... | collective-permute-start | bytes 196616 | tf_op jit(solution)/shard_map/ppermute | solution.py:227
  11.6 4.6 %collective-permute-start.6 = (bf16[512,128]{1,0:T(8,128)(2,1)S(1)}, bf16[512,128]{1,0:T(8,128)(2,1)S(1)}, u32[]{:S(2)}, u32[]{:S(2)}) collective-permute-start(bf16[512,128]{1,0:T(8,128)(2,1)S(1)} %constant_dynamic-update-slice_fusion.near), channel_id=1, source_target_pairs={{0,4},{1,5},{2,6},{3,7},{4,0},{5,1},{6,2},{7,3},{8,12},{9,13},{10,... | collective-permute-start | bytes 393224 | tf_op jit(solution)/shard_map/ppermute | solution.py:227
  11.7 3.6 %collective-permute-start.5 = (bf16[256,128]{1,0:T(8,128)(2,1)S(1)}, bf16[256,128]{1,0:T(8,128)(2,1)S(1)}, u32[]{:S(2)}, u32[]{:S(2)}) collective-permute-start(bf16[256,128]{1,0:T(8,128)(2,1)S(1)} %collective-permute-done.1.near), channel_id=1, source_target_pairs={{0,4},{1,5},{2,6},{3,7},{4,0},{5,1},{6,2},{7,3},{8,12},{9,13},{10,... | collective-permute-start | bytes 196616 | tf_op jit(solution)/shard_map/ppermute | solution.py:227
  12.2 1.2 %copy-start = (bf16[512,8,1,128]{3,1,2,0:T(8,128)(2,1)S(1)}, bf16[512,8,1,128]{3,1,2,0:T(8,128)(2,1)}, u32[]{:S(2)}) copy-start(bf16[512,8,1,128]{3,1,2,0:T(8,128)(2,1)} %param.4) | copy-start | bytes 3145732
  17.1 5.2 %collective-permute-start.7 = (bf16[256,128]{1,0:T(8,128)(2,1)S(1)}, bf16[256,128]{1,0:T(8,128)(2,1)S(1)}, u32[]{:S(2)}, u32[]{:S(2)}) collective-permute-start(bf16[256,128]{1,0:T(8,128)(2,1)S(1)} %get-tuple-element.26), channel_id=1, source_target_pairs={{0,24},{1,25},{2,26},{3,27},{4,7},{5,6},{6,5},{7,4},{8,16},{9,17},... | collective-permute-start | bytes 196616 | tf_op jit(solution)/shard_map/ppermute | solution.py:227
  19.2 4.3 %collective-permute-start.8 = (bf16[256,128]{1,0:T(8,128)(2,1)S(1)}, bf16[256,128]{1,0:T(8,128)(2,1)S(1)}, u32[]{:S(2)}, u32[]{:S(2)}) collective-permute-start(bf16[256,128]{1,0:T(8,128)(2,1)S(1)} %get-tuple-element.27), channel_id=1, source_target_pairs={{0,16},{1,17},{2,18},{3,19},{4,6},{5,7},{6,4},{7,5},{8,24},{9,25},... | collective-permute-start | bytes 196616 | tf_op jit(solution)/shard_map/ppermute | solution.py:227
  19.7 4.3 %collective-permute-start.9 = (bf16[256,128]{1,0:T(8,128)(2,1)S(1)}, bf16[256,128]{1,0:T(8,128)(2,1)S(1)}, u32[]{:S(2)}, u32[]{:S(2)}) collective-permute-start(bf16[256,128]{1,0:T(8,128)(2,1)S(1)} %get-tuple-element.28), channel_id=1, source_target_pairs={{0,8},{1,9},{2,10},{3,11},{4,5},{5,4},{6,7},{7,6},{8,0},{9,1},{10,... | collective-permute-start | bytes 196616 | tf_op jit(solution)/shard_map/ppermute | solution.py:227
  24.0 1.3 %collective-permute-start.10 = (bf16[128,128]{1,0:T(8,128)(2,1)S(1)}, bf16[128,128]{1,0:T(8,128)(2,1)S(1)}, u32[]{:S(2)}, u32[]{:S(2)}) collective-permute-start(bf16[128,128]{1,0:T(8,128)(2,1)S(1)} %get-tuple-element.30), channel_id=1, source_target_pairs={{0,4},{1,5},{2,6},{3,7},{4,0},{5,1},{6,2},{7,3},{8,12},{9,13},{10,... | collective-permute-start | bytes 98312 | tf_op jit(solution)/shard_map/ppermute | solution.py:227

commit v6 on v4

--- a/solution.py
+++ b/solution.py
@@ -49,6 +49,13 @@
             at = 1 - at
 
 
+ORDERS = ((2, 3, 1), (2, 3, 1))
+
+
+def distance_of(steps, side, k):
+    return ORDERS[side][k - 1] if steps == 3 else steps + 1 - k
+
+
 class Layout:
     def __init__(self, lines, planes, pts, width):
         self.lines, self.planes, self.pts, self.width = lines, planes, pts, width
@@ -64,7 +71,7 @@
 
     def blocks(self, side, lo, hi):
         n = (self.planes, self.lines)[side]
-        return [k for k in range(lo, hi) if k == 0 or self.steps + 1 - k < n]
+        return [k for k in range(lo, hi) if k == 0 or distance_of(self.steps, side, k) < n]
 
     def groups(self, side, lo, hi):
         have = self.blocks(side, lo, hi)
@@ -99,7 +106,7 @@
 
             def chip_of(side, k, line=line, plane=plane):
                 here, n = ((plane, self.planes), (line, self.lines))[side]
-                return origin(here, self.steps + 1 - k, n) if k else here
+                return origin(here, distance_of(self.steps, side, k), n) if k else here
 
             @pl.when(core == c)
             def _(c=c, chip_of=chip_of):
@@ -231,12 +238,12 @@
         return permute(value, lambda r, c: (r ^ 1, c))
 
     def exchange(value, k, to):
-        distance = steps + 1 - k
+        over_row, over_col = (distance_of(steps, side, k) for side in (0, 1))
 
         def target(r, c):
             if r % 2:
-                return r, to(c, (distance - 1) % (lines - 1) + 1, lines)
-            return 2 * to(r // 2, (distance - 1) % (planes - 1) + 1, planes), c
+                return r, to(c, (over_col - 1) % (lines - 1) + 1, lines)
+            return 2 * to(r // 2, (over_row - 1) % (planes - 1) + 1, planes), c
 
         return permute(value, target)
 

time: 26.1 us -> 26.3 us (level)
  waiting for transfers between devices: 9.52 us -> 9.84 us
    ppermute x11, waiting for transfers between devices: 9.52 us -> 9.84 us  [permute(): return lax.ppermute(value, AXES, pairs)]
where the time goes in v6:
time: 26.3 us; the launch traced here: 26.1 us
  waiting for transfers between devices  9.84 us (37%)
  starting transfers between devices  9.26 us (35%)
  Pallas kernels  4.18 us (16%)
  local copies, waits for them, and re-layouts  2.04 us (8%)
  other arithmetic  0.64 us (2%)
    ppermute x11, waiting for transfers between devices, permute(): return lax.ppermute(value, AXES, pairs)  9.84 us
    ppermute x11, starting transfers between devices, permute(): return lax.ppermute(value, AXES, pairs)  9.26 us
    pallas_call x5, Pallas kernels, call(): pl.pallas_call(body, out_shape=[jax.ShapeDtypeStruct(s, t) for s, t in ou...  3.19 us
    unnamed x5, local copies, waits for them, and re-layouts  1.23 us
    pallas_call x1, Pallas kernels, local_part(): pl.pallas_call(lambda *refs: relayout(wide, deep, *refs), out_shape=[jax....  0.99 us
    dynamic_update_slice x1, local copies, waits for them, and re-layouts, local_part(): lax.dynamic_update_slice(jnp.zeros((chip_rows, width), points.dtype), poi...  0.77 us
    add x1, other arithmetic, local_part(): return keep + swap(send)  0.64 us
  transfers between devices with their start and end apart: 11, of which 7 were waited for; matrix products, arithmetic and copies ran while one was open for 3% of the time, Pallas kernels for 13%

profile of v6, /device:TPU:0, one launch (start us, length us, event | category | flops | bytes accessed | tf_op | source)
XLA Modules:
  0.0 26.1 jit_solution(11628006784021185029)
XLA Ops:
  0.0 0.0 copy-start.1
  0.0 0.5 %collective-permute-start.2 = (bf16[512,8,1,128]{3,1,2,0:T(8,128)(2,1)}, bf16[512,8,1,128]{3,1,2,0:T(8,128)(2,1)S(1)}, u32[]{:S(2)}, u32[]{:S(2)}) collective-permute-start(bf16[512,8,1,128]{3,1,2,0:T(8,128)(2,1)} %param.4), channel_id=1, source_target_pairs={{0,4},{1,5},{2,6},{3,7},{4,0},{5,1},{6,2},{7,3},{8,12},{9,13},{10,... | collective-permute-start | bytes 3145736 | tf_op jit(solution)/shard_map/ppermute | solution.py:235
  0.5 0.1 collective-permute-start
  0.6 0.8 %constant_dynamic-update-slice_fusion.3 = bf16[256,128]{1,0:T(8,128)(2,1)S(1)} fusion(bf16[256,128]{1,0:T(8,128)(2,1)S(1)} %broadcast_in_dim.7, bf16[128,128]{1,0:T(8,128)(2,1)} %param.3, s32[]{:T(128)S(6)} %select_n.14), kind=kLoop, calls=%fused_computation.3 | loop fusion | bytes 65540 | tf_op jit(solution)/shard_map/dynamic_update_slice | solution.py:269
  1.3 1.7 %collective-permute-done = bf16[128,128]{1,0:T(8,128)(2,1)S(1)} collective-permute-done((bf16[128,128]{1,0:T(8,128)(2,1)}, bf16[128,128]{1,0:T(8,128)(2,1)S(1)}, u32[]{:S(2)}, u32[]{:S(2)}) %collective-permute-start) | collective-permute-done | bytes 32800 | tf_op jit(solution)/shard_map/ppermute | solution.py:235
  3.0 3.8 %collective-permute-start.3 = (bf16[256,128]{1,0:T(8,128)(2,1)S(1)}, bf16[256,128]{1,0:T(8,128)(2,1)S(1)}, u32[]{:S(2)}, u32[]{:S(2)}) collective-permute-start(bf16[256,128]{1,0:T(8,128)(2,1)S(1)} %constant_dynamic-update-slice_fusion.2.chip), channel_id=1, source_target_pairs={{0,24},{1,25},{2,26},{3,27},{4,7},{5,6},{6,5},{7,4},{8,16},{9,17},... | collective-permute-start | bytes 196616 | tf_op jit(solution)/shard_map/ppermute | solution.py:235
  6.9 0.5 %collective-permute-start.1 = (bf16[256,128]{1,0:T(8,128)(2,1)S(1)}, bf16[256,128]{1,0:T(8,128)(2,1)S(1)}, u32[]{:S(2)}, u32[]{:S(2)}) collective-permute-start(bf16[256,128]{1,0:T(8,128)(2,1)S(1)} %constant_dynamic-update-slice_fusion.2.chip), channel_id=1, source_target_pairs={{0,16},{1,17},{2,18},{3,19},{4,6},{5,7},{6,4},{7,5},{8,24},{9,25},... | collective-permute-start | bytes 196616 | tf_op jit(solution)/shard_map/ppermute | solution.py:235
  7.4 0.1 collective-permute-start.4
  7.5 1.6 %collective-permute-done.3 = bf16[256,128]{1,0:T(8,128)(2,1)S(1)} collective-permute-done((bf16[256,128]{1,0:T(8,128)(2,1)S(1)}, bf16[256,128]{1,0:T(8,128)(2,1)S(1)}, u32[]{:S(2)}, u32[]{:S(2)}) %collective-permute-start.3) | collective-permute-done | bytes 65568 | tf_op jit(solution)/shard_map/ppermute | solution.py:235
  9.1 2.5 %collective-permute-done.4 = bf16[256,128]{1,0:T(8,128)(2,1)S(1)} collective-permute-done((bf16[256,128]{1,0:T(8,128)(2,1)S(1)}, bf16[256,128]{1,0:T(8,128)(2,1)S(1)}, u32[]{:S(2)}, u32[]{:S(2)}) %collective-permute-start.4) | collective-permute-done | bytes 65568 | tf_op jit(solution)/shard_map/ppermute | solution.py:235
  11.6 0.1 collective-permute-start.6
  11.7 0.0 collective-permute-done.1.near
  11.7 0.5 %collective-permute-start.5 = (bf16[256,128]{1,0:T(8,128)(2,1)S(1)}, bf16[256,128]{1,0:T(8,128)(2,1)S(1)}, u32[]{:S(2)}, u32[]{:S(2)}) collective-permute-start(bf16[256,128]{1,0:T(8,128)(2,1)S(1)} %collective-permute-done.1.near), channel_id=1, source_target_pairs={{0,4},{1,5},{2,6},{3,7},{4,0},{5,1},{6,2},{7,3},{8,12},{9,13},{10,... | collective-permute-start | bytes 196616 | tf_op jit(solution)/shard_map/ppermute | solution.py:235
  12.2 0.0 collective-permute-done.2
  12.2 0.0 copy-start
  12.2 1.2 %copy-done = bf16[512,8,1,128]{3,1,2,0:T(8,128)(2,1)S(1)} copy-done((bf16[512,8,1,128]{3,1,2,0:T(8,128)(2,1)S(1)}, bf16[512,8,1,128]{3,1,2,0:T(8,128)(2,1)}, u32[]{:S(2)}) %copy-start) | copy-done | bytes 1048600
  13.4 1.0 %relayout.1 = (f32[512,1024]{1,0:T(8,128)S(1)}, f32[512,1024]{1,0:T(8,128)S(1)}) custom-call(bf16[4096,128]{1,0:T(8,128)(2,1)S(1)} %bitcast.3, bf16[4096,128]{1,0:T(8,128)(2,1)S(1)} %bitcast.4), custom_call_target="tpu_custom_call" | custom-call | tf_op jit(solution)/shard_map/relayout/pallas_call | solution.py:280
  14.4 0.0 copy-done.1
  14.5 0.9 %shard_map.37 = (bf16[512,256]{1,0:T(8,128)(2,1)S(1)}, bf16[256,256]{1,0:T(8,128)(2,1)S(1)}, f32[512,128]{1,0:T(8,128)S(1)}) custom-call(bf16[256,128]{1,0:T(8,128)(2,1)S(1)} %constant_dynamic-update-slice_fusion.2.chip, f32[1,128]{1,0:T(1,128)S(1)} %bitcast.5, bf16[256,128]{1,0:T(8,128)(2,1)S(1)} %collective-permute-done.1.near, ...), custom_call_target="tpu_custom_call" | custom-call | tf_op jit(solution)/shard_map/pallas_call | solution.py:259
  15.4 0.0 collective-permute-done.5.far
  15.4 0.9 %shard_map.38 = (bf16[512,256]{1,0:T(8,128)(2,1)S(1)}, f32[512,128]{1,0:T(8,128)S(1)}, f32[512,128]{1,0:T(8,128)S(1)}) custom-call(f32[1,128]{1,0:T(1,128)S(1)} %bitcast.6, bf16[512,128]{1,0:T(8,128)(2,1)S(1)} %constant_dynamic-update-slice_fusion.near, bf16[256,128]{1,0:T(8,128)(2,1)S(1)} %collective-permute-done.5.far, ...), custom_call_target="tpu_custom_call" | custom-call | tf_op jit(solution)/shard_map/pallas_call | solution.py:259
  16.3 0.0 collective-permute-done.6.far
  16.3 0.8 %shard_map.39 = (bf16[512,256]{1,0:T(8,128)(2,1)S(1)}, bf16[256,128]{1,0:T(8,128)(2,1)S(1)}, bf16[256,128]{1,0:T(8,128)(2,1)S(1)}, bf16[256,128]{1,0:T(8,128)(2,1)S(1)}) custom-call(f32[1,128]{1,0:T(1,128)S(1)} %bitcast.7, bf16[512,128]{1,0:T(8,128)(2,1)S(1)} %collective-permute-done.6.far, bf16[512,256]{1,0:T(8,128)(2,1)S(1)} %get-tuple-element.21.mine0, ...), custom_call_target="tpu_custom_call" | custom-call | tf_op jit(solution)/shard_map/pallas_call | solution.py:259
  17.1 1.6 %collective-permute-start.7 = (bf16[256,128]{1,0:T(8,128)(2,1)S(1)}, bf16[256,128]{1,0:T(8,128)(2,1)S(1)}, u32[]{:S(2)}, u32[]{:S(2)}) collective-permute-start(bf16[256,128]{1,0:T(8,128)(2,1)S(1)} %get-tuple-element.28), channel_id=1, source_target_pairs={{0,16},{1,17},{2,18},{3,19},{4,6},{5,7},{6,4},{7,5},{8,24},{9,25},... | collective-permute-start | bytes 196616 | tf_op jit(solution)/shard_map/ppermute | solution.py:235
  18.7 1.1 %collective-permute-start.8 = (bf16[256,128]{1,0:T(8,128)(2,1)S(1)}, bf16[256,128]{1,0:T(8,128)(2,1)S(1)}, u32[]{:S(2)}, u32[]{:S(2)}) collective-permute-start(bf16[256,128]{1,0:T(8,128)(2,1)S(1)} %get-tuple-element.29), channel_id=1, source_target_pairs={{0,24},{1,25},{2,26},{3,27},{4,7},{5,6},{6,5},{7,4},{8,16},{9,17},... | collective-permute-start | bytes 196616 | tf_op jit(solution)/shard_map/ppermute | solution.py:235
  19.8 0.9 %collective-permute-start.9 = (bf16[256,128]{1,0:T(8,128)(2,1)S(1)}, bf16[256,128]{1,0:T(8,128)(2,1)S(1)}, u32[]{:S(2)}, u32[]{:S(2)}) collective-permute-start(bf16[256,128]{1,0:T(8,128)(2,1)S(1)} %get-tuple-element.30), channel_id=1, source_target_pairs={{0,8},{1,9},{2,10},{3,11},{4,5},{5,4},{6,7},{7,6},{8,0},{9,1},{10,... | collective-permute-start | bytes 196616 | tf_op jit(solution)/shard_map/ppermute | solution.py:235
  20.7 0.5 %shard_map.40.refs_1_ = f32[256,128]{1,0:T(8,128)S(1)} custom-call(bf16[512,256]{1,0:T(8,128)(2,1)S(1)} %get-tuple-element.21.mine0, f32[512,128]{1,0:T(8,128)S(1)} %get-tuple-element.24.first, bf16[512,256]{1,0:T(8,128)(2,1)S(1)} %get-tuple-element.27.theirs, f32[512,1024]{1,0:T(8,128)S(1)} %get-tuple-element.19.a_own, ...), custom_call_target="tpu_custom_call" | custom-call | tf_op jit(solution)/shard_map/pallas_call | solution.py:259
  21.2 0.2 collective-permute-done.7.refs_2_
  21.4 2.4 %collective-permute-done.8.refs_3_ = bf16[256,128]{1,0:T(8,128)(2,1)S(1)} collective-permute-done((bf16[256,128]{1,0:T(8,128)(2,1)S(1)}, bf16[256,128]{1,0:T(8,128)(2,1)S(1)}, u32[]{:S(2)}, u32[]{:S(2)}) %collective-permute-start.8) | collective-permute-done | bytes 65568 | tf_op jit(solution)/shard_map/ppermute | solution.py:235
  23.9 0.2 collective-permute-done.9.refs_4_
  24.1 0.1 collective-permute-start.10
  24.2 1.2 %collective-permute-done.10 = f32[128,128]{1,0:T(8,128)S(1)} collective-permute-done((f32[128,128]{1,0:T(8,128)S(1)}, f32[128,128]{1,0:T(8,128)S(1)}, u32[]{:S(2)}, u32[]{:S(2)}) %collective-permute-start.10) | collective-permute-done | bytes 65568 | tf_op jit(solution)/shard_map/ppermute | solution.py:235
  25.4 0.6 %add.16 = f32[128,128]{1,0:T(8,128)} add(f32[128,128]{1,0:T(8,128)S(1)} %get-tuple-element.31, f32[128,128]{1,0:T(8,128)S(1)} %collective-permute-done.10) | non-fusion elementwise | flops 16384 | bytes 196608 | tf_op jit(solution)/shard_map/add | solution.py:335
  (5 shorter events, 0.1 us)
Async XLA Ops:
  0.0 14.4 %copy-start.1 = (f32[128]{0:T(128)S(1)}, f32[128]{0:T(128)}, u32[]{:S(2)}) copy-start(f32[128]{0:T(128)} %param.5) | copy-start | bytes 1540
  0.0 12.2 %collective-permute-start.2 = (bf16[512,8,1,128]{3,1,2,0:T(8,128)(2,1)}, bf16[512,8,1,128]{3,1,2,0:T(8,128)(2,1)S(1)}, u32[]{:S(2)}, u32[]{:S(2)}) collective-permute-start(bf16[512,8,1,128]{3,1,2,0:T(8,128)(2,1)} %param.4), channel_id=1, source_target_pairs={{0,4},{1,5},{2,6},{3,7},{4,0},{5,1},{6,2},{7,3},{8,12},{9,13},{10,... | collective-permute-start | bytes 3145736 | tf_op jit(solution)/shard_map/ppermute | solution.py:235
  0.5 2.5 %collective-permute-start = (bf16[128,128]{1,0:T(8,128)(2,1)}, bf16[128,128]{1,0:T(8,128)(2,1)S(1)}, u32[]{:S(2)}, u32[]{:S(2)}) collective-permute-start(bf16[128,128]{1,0:T(8,128)(2,1)} %param.3), channel_id=1, source_target_pairs={{0,4},{1,5},{2,6},{3,7},{4,0},{5,1},{6,2},{7,3},{8,12},{9,13},{10,... | collective-permute-start | bytes 98312 | tf_op jit(solution)/shard_map/ppermute | solution.py:235
  3.0 6.0 %collective-permute-start.3 = (bf16[256,128]{1,0:T(8,128)(2,1)S(1)}, bf16[256,128]{1,0:T(8,128)(2,1)S(1)}, u32[]{:S(2)}, u32[]{:S(2)}) collective-permute-start(bf16[256,128]{1,0:T(8,128)(2,1)S(1)} %constant_dynamic-update-slice_fusion.2.chip), channel_id=1, source_target_pairs={{0,24},{1,25},{2,26},{3,27},{4,7},{5,6},{6,5},{7,4},{8,16},{9,17},... | collective-permute-start | bytes 196616 | tf_op jit(solution)/shard_map/ppermute | solution.py:235
  6.9 4.9 %collective-permute-start.1 = (bf16[256,128]{1,0:T(8,128)(2,1)S(1)}, bf16[256,128]{1,0:T(8,128)(2,1)S(1)}, u32[]{:S(2)}, u32[]{:S(2)}) collective-permute-start(bf16[256,128]{1,0:T(8,128)(2,1)S(1)} %constant_dynamic-update-slice_fusion.2.chip), channel_id=1, source_target_pairs={{0,16},{1,17},{2,18},{3,19},{4,6},{5,7},{6,4},{7,5},{8,24},{9,25},... | collective-permute-start | bytes 196616 | tf_op jit(solution)/shard_map/ppermute | solution.py:235
  7.4 4.3 %collective-permute-start.4 = (bf16[256,128]{1,0:T(8,128)(2,1)S(1)}, bf16[256,128]{1,0:T(8,128)(2,1)S(1)}, u32[]{:S(2)}, u32[]{:S(2)}) collective-permute-start(bf16[256,128]{1,0:T(8,128)(2,1)S(1)} %constant_dynamic-update-slice_fusion.2.chip), channel_id=1, source_target_pairs={{0,8},{1,9},{2,10},{3,11},{4,5},{5,4},{6,7},{7,6},{8,0},{9,1},{10,... | collective-permute-start | bytes 196616 | tf_op jit(solution)/shard_map/ppermute | solution.py:235
  11.6 4.6 %collective-permute-start.6 = (bf16[512,128]{1,0:T(8,128)(2,1)S(1)}, bf16[512,128]{1,0:T(8,128)(2,1)S(1)}, u32[]{:S(2)}, u32[]{:S(2)}) collective-permute-start(bf16[512,128]{1,0:T(8,128)(2,1)S(1)} %constant_dynamic-update-slice_fusion.near), channel_id=1, source_target_pairs={{0,4},{1,5},{2,6},{3,7},{4,0},{5,1},{6,2},{7,3},{8,12},{9,13},{10,... | collective-permute-start | bytes 393224 | tf_op jit(solution)/shard_map/ppermute | solution.py:235
  11.7 3.6 %collective-permute-start.5 = (bf16[256,128]{1,0:T(8,128)(2,1)S(1)}, bf16[256,128]{1,0:T(8,128)(2,1)S(1)}, u32[]{:S(2)}, u32[]{:S(2)}) collective-permute-start(bf16[256,128]{1,0:T(8,128)(2,1)S(1)} %collective-permute-done.1.near), channel_id=1, source_target_pairs={{0,4},{1,5},{2,6},{3,7},{4,0},{5,1},{6,2},{7,3},{8,12},{9,13},{10,... | collective-permute-start | bytes 196616 | tf_op jit(solution)/shard_map/ppermute | solution.py:235
  12.2 1.2 %copy-start = (bf16[512,8,1,128]{3,1,2,0:T(8,128)(2,1)S(1)}, bf16[512,8,1,128]{3,1,2,0:T(8,128)(2,1)}, u32[]{:S(2)}) copy-start(bf16[512,8,1,128]{3,1,2,0:T(8,128)(2,1)} %param.4) | copy-start | bytes 3145732
  17.1 4.3 %collective-permute-start.7 = (bf16[256,128]{1,0:T(8,128)(2,1)S(1)}, bf16[256,128]{1,0:T(8,128)(2,1)S(1)}, u32[]{:S(2)}, u32[]{:S(2)}) collective-permute-start(bf16[256,128]{1,0:T(8,128)(2,1)S(1)} %get-tuple-element.28), channel_id=1, source_target_pairs={{0,16},{1,17},{2,18},{3,19},{4,6},{5,7},{6,4},{7,5},{8,24},{9,25},... | collective-permute-start | bytes 196616 | tf_op jit(solution)/shard_map/ppermute | solution.py:235
  18.7 5.2 %collective-permute-start.8 = (bf16[256,128]{1,0:T(8,128)(2,1)S(1)}, bf16[256,128]{1,0:T(8,128)(2,1)S(1)}, u32[]{:S(2)}, u32[]{:S(2)}) collective-permute-start(bf16[256,128]{1,0:T(8,128)(2,1)S(1)} %get-tuple-element.29), channel_id=1, source_target_pairs={{0,24},{1,25},{2,26},{3,27},{4,7},{5,6},{6,5},{7,4},{8,16},{9,17},... | collective-permute-start | bytes 196616 | tf_op jit(solution)/shard_map/ppermute | solution.py:235
  19.8 4.3 %collective-permute-start.9 = (bf16[256,128]{1,0:T(8,128)(2,1)S(1)}, bf16[256,128]{1,0:T(8,128)(2,1)S(1)}, u32[]{:S(2)}, u32[]{:S(2)}) collective-permute-start(bf16[256,128]{1,0:T(8,128)(2,1)S(1)} %get-tuple-element.30), channel_id=1, source_target_pairs={{0,8},{1,9},{2,10},{3,11},{4,5},{5,4},{6,7},{7,6},{8,0},{9,1},{10,... | collective-permute-start | bytes 196616 | tf_op jit(solution)/shard_map/ppermute | solution.py:235
  24.1 1.3 %collective-permute-start.10 = (f32[128,128]{1,0:T(8,128)S(1)}, f32[128,128]{1,0:T(8,128)S(1)}, u32[]{:S(2)}, u32[]{:S(2)}) collective-permute-start(f32[128,128]{1,0:T(8,128)S(1)} %get-tuple-element.32), channel_id=1, source_target_pairs={{0,4},{1,5},{2,6},{3,7},{4,0},{5,1},{6,2},{7,3},{8,12},{9,13},{10,... | collective-permute-start | bytes 196616 | tf_op jit(solution)/shard_map/ppermute | solution.py:235
